TPU v7x, 256 devices: a whole 4x4x8 slice. The times are simulated.
256 devices in a mesh: grp: 4 (over z_lo), tp: 32 (over x, y, z_hi), rep: 2 (over core).
Axes of the slice: x: 4, y: 4, z: 8 (z_hi: 2, z_lo: 4; z = z_hi * 4 + z_lo), core: 2. Of those that a mesh axis runs over, the one named last changes fastest.
Arguments:
- query_rows: bfloat16 [32, 1024, 2048], P('tp', ('grp', 'rep')), may hold values from -120 to 120
- key_rows: bfloat16 [32, 1024, 512], P('tp', ('grp', 'rep')), may hold values from -6 to 6, as said below
- value_rows: bfloat16 [32, 1024, 512], P('tp', ('grp', 'rep')), may hold values from -6 to 6
- teacher_codes: bfloat16 [32, 1024, 4096], P(None, ('grp', 'rep'), 'tp'), may hold values from -6 to 6
- teacher_scales: bfloat16 [32, 1024, 32], P(None, ('grp', 'rep'), 'tp'), may hold values from 0.099609375 to 1
- projection: bfloat16 [2048, 4096], P(None, ('grp', 'rep')), may hold values from -0.125 to 0.125
Outputs:
- grad_query: bfloat16 [32, 1024, 2048], P('tp', ('grp', 'rep'))
- grad_key: bfloat16 [32, 1024, 512], P('tp', ('grp', 'rep'))
- grad_value: bfloat16 [32, 1024, 512], P('tp', ('grp', 'rep'))
Inputs may be any that keep to these rules, and one draw needn't show every extreme that they name: `key_rows`: keys of every head.
All inputs are finite; a program needn't handle non-finite values.
Results may differ from a plain program's by a relative error of at most 0.014.
Values may be sent and summed in bfloat16 or wider, within the bound.
No kernel may reach another device: no remote copies, remote signals or barrier semaphores. Data moves between devices by JAX's collectives and lax.ppermute only.
A program may use at most 128 MiB of HBM per device.

v0:
```python
import math

import jax
import jax.numpy as jnp
from jax import lax
from jax.experimental import pallas as pl
from jax.experimental.pallas import tpu as pltpu
from jax.sharding import PartitionSpec as P


HEADS = 16
KV_HEADS = 4
GROUP = HEADS // KV_HEADS
HD = 128
ROWS = 128
FEAT = HEADS * HD
INV_ROOT = 1.0 / math.sqrt(HD)
LOW = -1e30
N_GRP = 4
SLOTS = 8
QUARTER = FEAT // 4
EIGHTH = FEAT // 8


SWAP = [(0, 1), (1, 0)]


def tp_of(x, y, zh):
    return x * 8 + y * 2 + zh


def x_shift(d):
    return [(tp_of(x, y, h), tp_of((x + d) % 4, y, h)) for x in range(4) for y in range(4) for h in range(2)]


def y_shift(d):
    return [(tp_of(x, y, h), tp_of(x, (y + d) % 4, h)) for x in range(4) for y in range(4) for h in range(2)]


X_PAIR = [(t, t ^ 8) for t in range(32)]
Y_PAIR = [(t, t ^ 2) for t in range(32)]


def z_shift(d):
    def at(x, y, z):
        return (z % 4) * 32 + tp_of(x, y, z // 4)

    return [(at(x, y, z), at(x, y, (z + d) % 8)) for x in range(4) for y in range(4) for z in range(8)]


def up(d):
    return [(i, i + d) for i in range(N_GRP - d)]


def down(d):
    return [(i + d, i) for i in range(N_GRP - d)]


def nt(a, b):
    return lax.dot_general(a, b, (((1,), (1,)), ((), ())), preferred_element_type=jnp.float32)


def nn(a, b):
    return lax.dot_general(a, b, (((1,), (0,)), ((), ())), preferred_element_type=jnp.float32)


def tn(a, b):
    return lax.dot_general(a, b, (((0,), (0,)), ((), ())), preferred_element_type=jnp.float32)


def stack_heads(block):
    return jnp.concatenate([block[:, g * HD : (g + 1) * HD] for g in range(GROUP)], axis=0)


def spread_heads(rows):
    return jnp.concatenate([rows[g * ROWS : (g + 1) * ROWS] for g in range(GROUP)], axis=1)


def forward_body(info, q, *refs):
    pieces, (wide, low, probs) = refs[:SLOTS], refs[SLOTS:]
    grp, rep = info[0], info[1]
    q4 = stack_heads(q[...])
    keys = jnp.concatenate([p[0] for p in pieces], axis=0)
    values = jnp.concatenate([p[1] for p in pieces], axis=0)
    scores = nt(q4, keys) * INV_ROOT
    row = lax.broadcasted_iota(jnp.int32, (GROUP * ROWS, ROWS), 0) % ROWS
    col = lax.broadcasted_iota(jnp.int32, (GROUP * ROWS, ROWS), 1)
    parts = []
    for s in range(SLOTS):
        d = s // 2
        part = scores[:, s * ROWS : (s + 1) * ROWS]
        if s == 0:
            part = jnp.where(col <= row, part, LOW)
        else:
            seen = rep == 1 if s == 1 else grp >= d
            part = jnp.where(seen, part, LOW)
        parts.append(part)
    scores = jnp.concatenate(parts, axis=1)
    peak = scores.max(axis=1, keepdims=True)
    shifted = jnp.exp(scores - peak)
    total = shifted.sum(axis=1, keepdims=True)
    prob_low = (shifted * (1.0 / total)).astype(jnp.bfloat16)
    probs[...] = prob_low
    out = spread_heads(nn(prob_low, values))
    wide[...] = out
    low[...] = out.astype(jnp.bfloat16)


def forward(info, q, pieces):
    return pl.pallas_call(
        forward_body,
        grid_spec=pltpu.PrefetchScalarGridSpec(
            num_scalar_prefetch=1,
            grid=(KV_HEADS,),
            in_specs=[pl.BlockSpec((ROWS, GROUP * HD), lambda h, i: (0, h))]
            + [pl.BlockSpec((2, ROWS, HD), lambda h, i: (0, 0, h))] * SLOTS,
            out_specs=[
                pl.BlockSpec((ROWS, GROUP * HD), lambda h, i: (0, h)),
                pl.BlockSpec((ROWS, GROUP * HD), lambda h, i: (0, h)),
                pl.BlockSpec((None, GROUP * ROWS, SLOTS * ROWS), lambda h, i: (h, 0, 0)),
            ],
        ),
        out_shape=[
            jax.ShapeDtypeStruct((ROWS, FEAT), jnp.float32),
            jax.ShapeDtypeStruct((ROWS, FEAT), jnp.bfloat16),
            jax.ShapeDtypeStruct((KV_HEADS, GROUP * ROWS, SLOTS * ROWS), jnp.bfloat16),
        ],
        cost_estimate=pl.CostEstimate(flops=10**10, bytes_accessed=8 * 10**6, transcendentals=2 * 10**6),
        name="attn_fwd",
    )(info, q, *pieces)


def project_body(info, mine, theirs, target_mine, target_theirs, own, *refs):
    arrays, (part_mine, part_theirs), (weights, both, acc, sems) = refs[:8], refs[8:10], refs[10:]
    grp, rep, xi, yi, zh = info[0], info[1], info[2], info[3], info[4]
    copies = [pltpu.make_async_copy(own, weights.at[3], sems.at[16])]
    copies[0].start()
    for a in range(8):
        half, far = a // 4, a % 4
        part = ((xi if half else yi) + 4 - far) % 4
        for k in range(2):
            sub = ((yi if half else xi) + k) % 2
            rows = pl.ds(pl.multiple_of(part * QUARTER + sub * EIGHTH, EIGHTH), EIGHTH)
            c = pltpu.make_async_copy(
                arrays[a].at[k], weights.at[pl.ds(0, 3), rows, pl.ds(half * 256, 256)], sems.at[2 * a + k]
            )
            c.start()
            copies.append(c)
    both[0:ROWS] = mine[...]
    both[ROWS:] = theirs[...]
    for n, (j, shift) in enumerate(((3, 0), (0, 3), (1, 1), (2, 2))):
        if n == 0:
            copies[0].wait()
        if n == 1:
            for c in copies[1:]:
                c.wait()
        block = (grp + shift) % 4
        approx = nn(both[...], weights[j])
        target = jnp.concatenate(
            [
                jnp.concatenate(
                    [target_mine[(c + zh) % 2, block, rep, c // 2], target_theirs[(c + zh) % 2, block, c // 2]], axis=0
                )
                for c in range(4)
            ],
            axis=1,
        )
        errors = (approx - target.astype(jnp.float32)).astype(jnp.bfloat16)
        term = nt(errors, weights[j])
        if n == 0:
            acc[...] = term
        else:
            acc[...] += term
    part_mine[...] = acc[0:ROWS]
    part_theirs[...] = acc[ROWS:].astype(jnp.bfloat16)


def project(info, mine, theirs, target_mine, target_theirs, own, arrays):
    vmem = pl.BlockSpec(memory_space=pltpu.VMEM)
    hbm = pl.BlockSpec(memory_space=pltpu.HBM)
    return pl.pallas_call(
        project_body,
        grid_spec=pltpu.PrefetchScalarGridSpec(
            num_scalar_prefetch=1,
            grid=(1,),
            in_specs=[vmem] * 4 + [hbm] * 9,
            out_specs=[vmem, vmem],
            scratch_shapes=[
                pltpu.VMEM((4, FEAT, 512), jnp.bfloat16),
                pltpu.VMEM((2 * ROWS, FEAT), jnp.bfloat16),
                pltpu.VMEM((2 * ROWS, FEAT), jnp.float32),
                pltpu.SemaphoreType.DMA((17,)),
            ],
        ),
        out_shape=[
            jax.ShapeDtypeStruct((ROWS, FEAT), jnp.float32),
            jax.ShapeDtypeStruct((ROWS, FEAT), jnp.bfloat16),
        ],
        cost_estimate=pl.CostEstimate(flops=10**10, bytes_accessed=12 * 10**6, transcendentals=0),
        name="project",
    )(info, mine, theirs, target_mine, target_theirs, own, *arrays)


def backward_body(probs, part, got, wide, q, *refs):
    pieces, (grad_q, terms_mine, terms_theirs) = refs[:SLOTS], refs[SLOTS:]
    grad = (part[...] + got[...].astype(jnp.float32)).astype(jnp.bfloat16)
    delta = stack_heads(grad.astype(jnp.float32) * wide[...]).sum(axis=1, keepdims=True)
    g4 = stack_heads(grad)
    q4 = stack_heads(q[...])
    keys = jnp.concatenate([p[0] for p in pieces], axis=0)
    values = jnp.concatenate([p[1] for p in pieces], axis=0)
    p_low = probs[...]
    grad_prob = nt(g4, values)
    grad_score = (p_low.astype(jnp.float32) * (grad_prob - delta) * INV_ROOT).astype(jnp.bfloat16)
    grad_q[...] = spread_heads(nn(grad_score, keys)).astype(jnp.bfloat16)
    key_terms = tn(grad_score, q4).astype(jnp.bfloat16)
    value_terms = tn(p_low, g4).astype(jnp.bfloat16)
    for s in range(SLOTS):
        out = terms_theirs if s % 2 else terms_mine
        out[s // 2, 0] = key_terms[s * ROWS : (s + 1) * ROWS]
        out[s // 2, 1] = value_terms[s * ROWS : (s + 1) * ROWS]


def backward(probs, part, got, wide, q, pieces):
    rows = pl.BlockSpec((ROWS, GROUP * HD), lambda h: (0, h))
    terms = pl.BlockSpec((N_GRP, 2, ROWS, HD), lambda h: (0, 0, 0, h))
    return pl.pallas_call(
        backward_body,
        grid=(KV_HEADS,),
        in_specs=[pl.BlockSpec((None, GROUP * ROWS, SLOTS * ROWS), lambda h: (h, 0, 0)), rows, rows, rows, rows]
        + [pl.BlockSpec((2, ROWS, HD), lambda h: (0, 0, h))] * SLOTS,
        out_specs=[rows, terms, terms],
        out_shape=[
            jax.ShapeDtypeStruct((ROWS, FEAT), jnp.bfloat16),
            jax.ShapeDtypeStruct((N_GRP, 2, ROWS, KV_HEADS * HD), jnp.bfloat16),
            jax.ShapeDtypeStruct((N_GRP, 2, ROWS, KV_HEADS * HD), jnp.bfloat16),
        ],
        cost_estimate=pl.CostEstimate(flops=10**10, bytes_accessed=8 * 10**6, transcendentals=0),
        name="attn_bwd",
    )(probs, part, got, wide, q, *pieces)


def spread_weights(projection, xi, yi):
    places = ((yi, xi % 2), (xi, yi % 2))
    parts = [
        lax.dynamic_slice(projection, (at * QUARTER + sub * EIGHTH, half * 256), (EIGHTH, 256))
        for half, (at, sub) in enumerate(places)
    ]
    below, above = [lax.ppermute(jnp.stack(parts), ("grp", "tp"), z_shift(d)) for d in (1, 7)]
    across = [lax.ppermute(part, ("grp", "tp"), z_shift(d)) for part, d in zip(parts, (2, 6))]
    arrays = []
    for half, (pair, far) in enumerate(((X_PAIR, y_shift), (Y_PAIR, x_shift))):
        slab = jnp.stack([below[half], above[half], across[half]])
        other = lax.ppermute(slab, "tp", pair)
        slab = jnp.stack([slab, other])
        arrays += [slab] + [lax.ppermute(slab, "tp", far(d)) for d in (1, 2, 3)]
    return arrays


def join_body(keys, values, out):
    out[0:1] = keys[...]
    out[1:2] = values[...]


def gather_keys(key_rows, value_rows, give):
    piece = pl.pallas_call(
        join_body, out_shape=jax.ShapeDtypeStruct((2, ROWS, KV_HEADS * HD), jnp.bfloat16), name="join"
    )(key_rows, value_rows)
    pieces = []
    for d in range(N_GRP):
        if d == 3:
            piece, give = lax.optimization_barrier((piece, give))
        if d:
            piece = lax.ppermute(piece, "grp", up(1))
        pieces += [piece, lax.ppermute(piece, "rep", SWAP)]
    return pieces, give


def step(query_rows, key_rows, value_rows, teacher_codes, teacher_scales, projection):
    grp, rep, tp = lax.axis_index("grp"), lax.axis_index("rep"), lax.axis_index("tp")
    xi, yi, zh = tp // 8, (tp // 2) % 4, tp % 2
    info = jnp.stack([grp, rep, xi, yi, zh]).astype(jnp.int32)
    query = query_rows[0]

    arrays = spread_weights(projection, xi, yi)
    rows = (teacher_codes.astype(jnp.float32) * teacher_scales.astype(jnp.float32)).astype(jnp.bfloat16)
    rows = rows.reshape(16, 2, ROWS, HD)
    rows = lax.all_to_all(
        rows,
        "tp",
        split_axis=0,
        concat_axis=0,
        tiled=True,
        axis_index_groups=[[2 * t + h for t in range(16)] for h in range(2)],
    )
    keep = lax.dynamic_index_in_dim(rows, zh, 1, keepdims=False)
    give = lax.dynamic_index_in_dim(rows, 1 - zh, 1, keepdims=False)
    pieces, give = gather_keys(key_rows, value_rows, give)
    got = lax.ppermute(give, "tp", [(t, t ^ 1) for t in range(32)])
    target_mine = jnp.stack([keep, got]).reshape(2, N_GRP, 2, 2, ROWS, HD)
    give = lax.dynamic_index_in_dim(target_mine, 1 - rep, 2, keepdims=False)
    target_theirs = lax.ppermute(give, "rep", SWAP)

    wide, low, probs = forward(info, query, pieces)
    theirs = lax.ppermute(low, "rep", SWAP)
    part, give = project(info, low, theirs, target_mine, target_theirs, projection, arrays)
    got = lax.ppermute(give, "rep", SWAP)
    grad_q, terms_mine, terms_theirs = backward(probs, part, got, wide, query, pieces)
    got = lax.ppermute(terms_theirs, "rep", SWAP)
    terms = [terms_mine[d].astype(jnp.float32) + got[d].astype(jnp.float32) for d in range(N_GRP)]
    low_terms = [t.astype(jnp.bfloat16) for t in terms]
    relayed = lax.ppermute(low_terms[3], "grp", [(3, 2)])
    near = lax.ppermute(low_terms[1], "grp", down(1))
    far = lax.ppermute(low_terms[2], "grp", [(3, 1)])
    joined = (terms[2] + relayed.astype(jnp.float32)).astype(jnp.bfloat16)
    joined = lax.ppermute(joined, "grp", [(2, 0)])
    total = terms[0] + near.astype(jnp.float32) + far.astype(jnp.float32) + joined.astype(jnp.float32)
    total = total.astype(jnp.bfloat16)
    return grad_q[None], total[0:1], total[1:2]


def solution(mesh):
    rows = P("tp", ("grp", "rep"), None)
    cols = P(None, ("grp", "rep"), "tp")
    return jax.shard_map(
        step,
        mesh=mesh,
        in_specs=(rows, rows, rows, cols, cols, P(None, ("grp", "rep"))),
        out_specs=(rows, rows, rows),
        check_vma=False,
    )
```

profile of v0, /device:TPU:4, one launch (start us, length us, event | category | flops | bytes accessed | tf_op | source)
XLA Modules:
  0.0 164.7 jit_solution(426684365096508747)
XLA Ops:
  0.7 1.0 constant_dynamic-slice_fusion.2
  1.7 3.3 %collective-permute-start.12 = (bf16[256,256]{1,0:T(8,128)(2,1)S(1)}, bf16[256,256]{1,0:T(8,128)(2,1)S(1)}, u32[]{:S(2)}, u32[]{:S(2)}) collective-permute-start(bf16[256,256]{1,0:T(8,128)(2,1)S(1)} %get-tuple-element.27), channel_id=1, source_target_pairs={{0,128},{64,192},{128,2},{192,66},{2,130},{66,194},{130,0},{194,64... | collective-permute-start | bytes 393224 | tf_op jit(solution)/shard_map/ppermute | solution.py:250
  5.1 2.7 %collective-permute-start.11 = (bf16[2,256,256]{2,1,0:T(8,128)(2,1)S(1)}, bf16[2,256,256]{2,1,0:T(8,128)(2,1)S(1)}, u32[]{:S(2)}, u32[]{:S(2)}) collective-permute-start(bf16[2,256,256]{2,1,0:T(8,128)(2,1)S(1)} %pad_maximum_fusion.5), channel_id=1, source_target_pairs={{0,194},{64,0},{128,64},{192,128},{2,192},{66,2},{130,66},{194,130... | collective-permute-start | bytes 786440 | tf_op jit(solution)/shard_map/ppermute | solution.py:249
  7.8 0.7 bitcast_convert_fusion.1
  8.5 2.5 %multiply_convert_fusion = bf16[32,128,128]{2,1,0:T(8,128)(2,1)} fusion(bf16[32,128,128]{2,1,0:T(8,128)(2,1)} %param.9, f32[32,128]{1,0:T(8,128)S(1)} %bitcast_convert_fusion.1), kind=kLoop, calls=%fused_computation | loop fusion | flops 1572864 | bytes 2113536 | tf_op jit(solution)/shard_map/convert_element_type | solution.py:286
  11.0 7.5 %all-to-all-start = ((bf16[16,2,128,128]{3,2,1,0:T(8,128)(2,1)}), bf16[16,2,128,128]{3,2,1,0:T(8,128)(2,1)S(1)}, u32[]{:S(2)}, u32[]{:S(2)}) async-start(bf16[16,2,128,128]{3,2,1,0:T(8,128)(2,1)} %bitcast.7), calls=%async_computation | async-start | bytes 2097152 | tf_op jit(solution)/shard_map/all_to_all | solution.py:288
  18.5 0.0 collective-permute-done.11
  18.5 1.1 collective-permute-done.10
  19.6 0.1 fusion.9
  19.7 1.3 collective-permute-start.13
  20.9 1.7 %join.1.refs_0_ = bf16[2,128,512]{2,1,0:T(8,128)(2,1)} custom-call(bf16[1,128,512]{2,1,0:T(8,128)(2,1)} %keys.1, bf16[1,128,512]{2,1,0:T(8,128)(2,1)} %values.1), custom_call_target="tpu_custom_call" | custom-call | tf_op jit(solution)/shard_map/join/pallas_call | solution.py:266
  22.6 4.2 %collective-permute-start.1 = (bf16[2,128,512]{2,1,0:T(8,128)(2,1)}, bf16[2,128,512]{2,1,0:T(8,128)(2,1)}, u32[]{:S(2)}, u32[]{:S(2)}) collective-permute-start(bf16[2,128,512]{2,1,0:T(8,128)(2,1)} %join.1.refs_0_), channel_id=1, source_target_pairs={{0,64},{64,128},{128,192},{1,65},{65,129},{129,193},{2,66},{66,130... | collective-permute-start | bytes 786440 | tf_op jit(solution)/shard_map/ppermute | solution.py:274
  26.8 1.5 collective-permute-start.17
  28.4 2.2 %collective-permute-done.1.refs_2_ = bf16[2,128,512]{2,1,0:T(8,128)(2,1)} collective-permute-done((bf16[2,128,512]{2,1,0:T(8,128)(2,1)}, bf16[2,128,512]{2,1,0:T(8,128)(2,1)}, u32[]{:S(2)}, u32[]{:S(2)}) %collective-permute-start.1) | collective-permute-done | bytes 262176 | tf_op jit(solution)/shard_map/ppermute | solution.py:274
  30.6 5.1 %collective-permute-start.3 = (bf16[2,128,512]{2,1,0:T(8,128)(2,1)}, bf16[2,128,512]{2,1,0:T(8,128)(2,1)}, u32[]{:S(2)}, u32[]{:S(2)}) collective-permute-start(bf16[2,128,512]{2,1,0:T(8,128)(2,1)} %collective-permute-done.1.refs_2_), channel_id=1, source_target_pairs={{0,64},{64,128},{128,192},{1,65},{65,129},{129,193},{2,66},{66,130... | collective-permute-start | bytes 786440 | tf_op jit(solution)/shard_map/ppermute | solution.py:274
  35.7 3.7 %collective-permute-done.13 = bf16[3,256,256]{2,1,0:T(8,128)(2,1)S(1)} collective-permute-done((bf16[3,256,256]{2,1,0:T(8,128)(2,1)S(1)}, bf16[3,256,256]{2,1,0:T(8,128)(2,1)S(1)}, u32[]{:S(2)}, u32[]{:S(2)}) %collective-permute-start.13) | collective-permute-done | bytes 393248 | tf_op jit(solution)/shard_map/ppermute | solution.py:254
  39.4 0.1 pad_maximum_fusion.1.refs_0_
  39.5 2.8 %collective-permute-start.16 = (bf16[2,3,256,256]{3,2,1,0:T(8,128)(2,1)S(1)}, bf16[2,3,256,256]{3,2,1,0:T(8,128)(2,1)}, u32[]{:S(2)}, u32[]{:S(2)}) collective-permute-start(bf16[2,3,256,256]{3,2,1,0:T(8,128)(2,1)S(1)} %pad_maximum_fusion.1.refs_0_), channel_id=1, source_target_pairs={{0,12},{2,14},{4,0},{6,2},{8,4},{10,6},{12,8},{14,10},{16,28},{18,... | collective-permute-start | bytes 2359304 | tf_op jit(solution)/shard_map/ppermute | solution.py:256
  42.2 0.0 collective-permute-done.17
  42.2 0.8 fusion.8
  43.1 0.0 collective-permute-start
  43.1 0.0 all-to-all-done
  43.1 0.9 constant_dynamic-slice_fusion.1
  44.0 0.0 collective-permute-done.3.refs_4_
  44.0 4.2 %collective-permute-start.5 = (bf16[2,128,512]{2,1,0:T(8,128)(2,1)}, bf16[2,128,512]{2,1,0:T(8,128)(2,1)S(1)}, u32[]{:S(2)}, u32[]{:S(2)}) collective-permute-start(bf16[2,128,512]{2,1,0:T(8,128)(2,1)} %collective-permute-done.3.refs_4_), channel_id=1, source_target_pairs={{0,64},{64,128},{128,192},{1,65},{65,129},{129,193},{2,66},{66,130... | collective-permute-start | bytes 786440 | tf_op jit(solution)/shard_map/ppermute | solution.py:274
  48.2 3.1 %collective-permute-start.8 = (bf16[16,128,128]{2,1,0:T(8,128)(2,1)}, bf16[16,128,128]{2,1,0:T(8,128)(2,1)S(1)}, u32[]{:S(2)}, u32[]{:S(2)}) collective-permute-start(bf16[16,128,128]{2,1,0:T(8,128)(2,1)} %get-tuple-element.16), channel_id=1, source_target_pairs={{0,2},{2,0},{4,6},{6,4},{8,10},{10,8},{12,14},{14,12},{16,18},{18,... | collective-permute-start | bytes 1572872 | tf_op jit(solution)/shard_map/ppermute | solution.py:299
  51.3 14.7 %collective-permute-done.18 = bf16[3,256,256]{2,1,0:T(8,128)(2,1)} collective-permute-done((bf16[3,256,256]{2,1,0:T(8,128)(2,1)}, bf16[3,256,256]{2,1,0:T(8,128)(2,1)}, u32[]{:S(2)}, u32[]{:S(2)}) %collective-permute-start.18) | collective-permute-done | bytes 393248 | tf_op jit(solution)/shard_map/ppermute | solution.py:254
  66.0 0.0 collective-permute-start.4
  66.0 0.0 collective-permute-done.5.refs_6_
  66.0 0.5 collective-permute-start.6
  66.5 0.6 stack.74.info
  67.1 1.1 pad_maximum_fusion.2.refs_4_
  68.2 0.0 collective-permute-done.2.refs_3_
  68.2 3.1 %collective-permute-start.15 = (bf16[2,3,256,256]{3,2,1,0:T(8,128)(2,1)S(1)}, bf16[2,3,256,256]{3,2,1,0:T(8,128)(2,1)}, u32[]{:S(2)}, u32[]{:S(2)}) collective-permute-start(bf16[2,3,256,256]{3,2,1,0:T(8,128)(2,1)S(1)} %pad_maximum_fusion.1.refs_0_), channel_id=1, source_target_pairs={{0,8},{2,10},{4,12},{6,14},{8,0},{10,2},{12,4},{14,6},{16,24},{18,... | collective-permute-start | bytes 2359304 | tf_op jit(solution)/shard_map/ppermute | solution.py:256
  71.2 0.0 collective-permute-done.4.refs_5_
  71.3 0.1 collective-permute-start.21
  71.4 2.9 %collective-permute-start.20 = (bf16[2,3,256,256]{3,2,1,0:T(8,128)(2,1)S(1)}, bf16[2,3,256,256]{3,2,1,0:T(8,128)(2,1)}, u32[]{:S(2)}, u32[]{:S(2)}) collective-permute-start(bf16[2,3,256,256]{3,2,1,0:T(8,128)(2,1)S(1)} %pad_maximum_fusion.2.refs_4_), channel_id=1, source_target_pairs={{0,32},{2,34},{4,36},{6,38},{8,40},{10,42},{12,44},{14,46},{16,48}... | collective-permute-start | bytes 2359304 | tf_op jit(solution)/shard_map/ppermute | solution.py:256
  74.3 0.6 collective-permute-start.19
  74.8 9.8 %attn_fwd.1 = (f32[128,2048]{1,0:T(8,128)}, bf16[128,2048]{1,0:T(8,128)(2,1)}, bf16[4,512,1024]{2,1,0:T(8,128)(2,1)}) custom-call(s32[5]{0:T(128)} %stack.74.info, bf16[128,2048]{1,0:T(8,128)(2,1)} %bitcast.53, bf16[2,128,512]{2,1,0:T(8,128)(2,1)} %join.1.refs_0_, bf16[2,128,512]{2,1,0:T(8,128)(2,1)} %collective-permute-done.refs_1_, ...), custom_call_target="tpu_custom_call" | custom-call | flops 10000000000 | bytes 8000000 | tf_op jit(solution)/shard_map/attn_fwd/pallas_call | solution.py:110
  84.7 0.1 fusion.1
  84.8 5.6 %collective-permute-done.15.refs_2_ = bf16[2,3,256,256]{3,2,1,0:T(8,128)(2,1)} collective-permute-done((bf16[2,3,256,256]{3,2,1,0:T(8,128)(2,1)S(1)}, bf16[2,3,256,256]{3,2,1,0:T(8,128)(2,1)}, u32[]{:S(2)}, u32[]{:S(2)}) %collective-permute-start.15) | collective-permute-done | bytes 786464 | tf_op jit(solution)/shard_map/ppermute | solution.py:256
  90.3 15.9 %collective-permute-done.14.refs_1_ = bf16[2,3,256,256]{3,2,1,0:T(8,128)(2,1)} collective-permute-done((bf16[2,3,256,256]{3,2,1,0:T(8,128)(2,1)S(1)}, bf16[2,3,256,256]{3,2,1,0:T(8,128)(2,1)}, u32[]{:S(2)}, u32[]{:S(2)}) %collective-permute-start.14) | collective-permute-done | bytes 786464 | tf_op jit(solution)/shard_map/ppermute | solution.py:256
  106.3 0.0 collective-permute-start.7
  106.3 1.1 pad_maximum_fusion.target_mine
  107.4 1.8 %collective-permute-done.19.refs_5_ = bf16[2,3,256,256]{3,2,1,0:T(8,128)(2,1)} collective-permute-done((bf16[2,3,256,256]{3,2,1,0:T(8,128)(2,1)S(1)}, bf16[2,3,256,256]{3,2,1,0:T(8,128)(2,1)}, u32[]{:S(2)}, u32[]{:S(2)}) %collective-permute-start.19) | collective-permute-done | bytes 786464 | tf_op jit(solution)/shard_map/ppermute | solution.py:256
  109.2 0.8 copy-done.4
  110.0 0.8 copy-done.5
  110.8 10.6 %project.1 = (f32[128,2048]{1,0:T(8,128)}, bf16[128,2048]{1,0:T(8,128)(2,1)}) custom-call(s32[5]{0:T(128)} %stack.74.info, bf16[128,2048]{1,0:T(8,128)(2,1)} %get-tuple-element.15.mine, bf16[128,2048]{1,0:T(8,128)(2,1)} %copy-done.5, bf16[2,4,2,2,128,128]{5,4,3,2,1,0:T(8,128)(2,1)} %pad_maximum_fusion.target_mine, bf16[2,4,2,128,128]{4,3,2,1,0:T(8,128)(2,1)} %copy-done.4, ...), custom_call_target="tpu_custom_call" | custom-call | flops 10000000000 | bytes 12000000 | tf_op jit(solution)/shard_map/project/pallas_call | solution.py:181
  121.4 0.1 collective-permute-start.22
  121.5 2.1 %collective-permute-done.22.got = bf16[128,2048]{1,0:T(8,128)(2,1)S(1)} collective-permute-done((bf16[128,2048]{1,0:T(8,128)(2,1)}, bf16[128,2048]{1,0:T(8,128)(2,1)S(1)}, u32[]{:S(2)}, u32[]{:S(2)}) %collective-permute-start.22) | collective-permute-done | bytes 524320 | tf_op jit(solution)/shard_map/ppermute | solution.py:307
  123.6 0.8 copy-done.6
  124.4 8.2 %attn_bwd.1 = (bf16[128,2048]{1,0:T(8,128)(2,1)}, bf16[4,2,128,512]{3,2,1,0:T(8,128)(2,1)}, bf16[4,2,128,512]{3,2,1,0:T(8,128)(2,1)}) custom-call(bf16[4,512,1024]{2,1,0:T(8,128)(2,1)} %get-tuple-element.14.probs, f32[128,2048]{1,0:T(8,128)} %get-tuple-element.17.part, bf16[128,2048]{1,0:T(8,128)(2,1)} %copy-done.6, f32[128,2048]{1,0:T(8,128)} %get-tuple-element.19.wide, ...), custom_call_target="tpu_custom_call" | custom-call | flops 10000000000 | bytes 8000000 | tf_op jit(solution)/shard_map/attn_bwd/pallas_call | solution.py:227
  132.6 0.2 collective-permute-start.23
  132.9 2.7 %collective-permute-done.23 = bf16[4,2,128,512]{3,2,1,0:T(8,128)(2,1)S(1)} collective-permute-done((bf16[4,2,128,512]{3,2,1,0:T(8,128)(2,1)}, bf16[4,2,128,512]{3,2,1,0:T(8,128)(2,1)S(1)}, u32[]{:S(2)}, u32[]{:S(2)}) %collective-permute-start.23) | collective-permute-done | bytes 1048608 | tf_op jit(solution)/shard_map/ppermute | solution.py:309
  135.6 1.3 fusion.6
  136.9 0.7 collective-permute-start.26
  137.6 1.3 collective-permute-start.24
  138.9 0.7 collective-permute-start.25
  139.6 0.1 fusion.2
  139.7 1.3 collective-permute-start.27
  141.0 7.2 %collective-permute-done.24 = bf16[2,128,512]{2,1,0:T(8,128)(2,1)S(1)} collective-permute-done((bf16[2,128,512]{2,1,0:T(8,128)(2,1)S(1)}, bf16[2,128,512]{2,1,0:T(8,128)(2,1)S(1)}, u32[]{:S(2)}, u32[]{:S(2)}) %collective-permute-start.24) | collective-permute-done | bytes 262176 | tf_op jit(solution)/shard_map/ppermute | solution.py:313
  148.2 15.6 %collective-permute-done.27 = bf16[2,128,512]{2,1,0:T(8,128)(2,1)S(1)} collective-permute-done((bf16[2,128,512]{2,1,0:T(8,128)(2,1)S(1)}, bf16[2,128,512]{2,1,0:T(8,128)(2,1)S(1)}, u32[]{:S(2)}, u32[]{:S(2)}) %collective-permute-start.27) | collective-permute-done | bytes 262176 | tf_op jit(solution)/shard_map/ppermute | solution.py:316
  163.8 0.2 fusion.5
  164.0 0.7 fusion.10
  (34 shorter events, 0.1 us)
Async XLA Ops:
  1.7 17.9 %collective-permute-start.12 = (bf16[256,256]{1,0:T(8,128)(2,1)S(1)}, bf16[256,256]{1,0:T(8,128)(2,1)S(1)}, u32[]{:S(2)}, u32[]{:S(2)}) collective-permute-start(bf16[256,256]{1,0:T(8,128)(2,1)S(1)} %get-tuple-element.27), channel_id=1, source_target_pairs={{0,128},{64,192},{128,2},{192,66},{2,130},{66,194},{130,0},{194,64... | collective-permute-start | bytes 393224 | tf_op jit(solution)/shard_map/ppermute | solution.py:250
  5.1 13.4 %collective-permute-start.11 = (bf16[2,256,256]{2,1,0:T(8,128)(2,1)S(1)}, bf16[2,256,256]{2,1,0:T(8,128)(2,1)S(1)}, u32[]{:S(2)}, u32[]{:S(2)}) collective-permute-start(bf16[2,256,256]{2,1,0:T(8,128)(2,1)S(1)} %pad_maximum_fusion.5), channel_id=1, source_target_pairs={{0,194},{64,0},{128,64},{192,128},{2,192},{66,2},{130,66},{194,130... | collective-permute-start | bytes 786440 | tf_op jit(solution)/shard_map/ppermute | solution.py:249
  7.8 11.8 %collective-permute-start.10 = (bf16[2,256,256]{2,1,0:T(8,128)(2,1)S(1)}, bf16[2,256,256]{2,1,0:T(8,128)(2,1)S(1)}, u32[]{:S(2)}, u32[]{:S(2)}) collective-permute-start(bf16[2,256,256]{2,1,0:T(8,128)(2,1)S(1)} %pad_maximum_fusion.5), channel_id=1, source_target_pairs={{0,64},{64,128},{128,192},{192,2},{2,66},{66,130},{130,194},{194,0... | collective-permute-start | bytes 786440 | tf_op jit(solution)/shard_map/ppermute | solution.py:249
  11.0 32.1 %all-to-all-start = ((bf16[16,2,128,128]{3,2,1,0:T(8,128)(2,1)}), bf16[16,2,128,128]{3,2,1,0:T(8,128)(2,1)S(1)}, u32[]{:S(2)}, u32[]{:S(2)}) async-start(bf16[16,2,128,128]{3,2,1,0:T(8,128)(2,1)} %bitcast.7), calls=%async_computation | async-start | bytes 2097152 | tf_op jit(solution)/shard_map/all_to_all | solution.py:288
  19.7 19.7 %collective-permute-start.13 = (bf16[3,256,256]{2,1,0:T(8,128)(2,1)S(1)}, bf16[3,256,256]{2,1,0:T(8,128)(2,1)S(1)}, u32[]{:S(2)}, u32[]{:S(2)}) collective-permute-start(bf16[3,256,256]{2,1,0:T(8,128)(2,1)S(1)} %get-tuple-element.33), channel_id=1, source_target_pairs={{0,16},{2,18},{4,20},{6,22},{8,24},{10,26},{12,28},{14,30},{16,0},... | collective-permute-start | bytes 1179656 | tf_op jit(solution)/shard_map/ppermute | solution.py:254
  22.6 20.4 %copy-start.3 = (bf16[2,128,512]{2,1,0:T(8,128)(2,1)S(1)}, bf16[2,128,512]{2,1,0:T(8,128)(2,1)}, u32[]{:S(2)}) copy-start(bf16[2,128,512]{2,1,0:T(8,128)(2,1)} %join.1.refs_0_) | copy-start | bytes 786436
  22.6 8.0 %collective-permute-start.1 = (bf16[2,128,512]{2,1,0:T(8,128)(2,1)}, bf16[2,128,512]{2,1,0:T(8,128)(2,1)}, u32[]{:S(2)}, u32[]{:S(2)}) collective-permute-start(bf16[2,128,512]{2,1,0:T(8,128)(2,1)} %join.1.refs_0_), channel_id=1, source_target_pairs={{0,64},{64,128},{128,192},{1,65},{65,129},{129,193},{2,66},{66,130... | collective-permute-start | bytes 786440 | tf_op jit(solution)/shard_map/ppermute | solution.py:274
  26.8 15.4 %collective-permute-start.17 = (bf16[256,256]{1,0:T(8,128)(2,1)S(1)}, bf16[256,256]{1,0:T(8,128)(2,1)S(1)}, u32[]{:S(2)}, u32[]{:S(2)}) collective-permute-start(bf16[256,256]{1,0:T(8,128)(2,1)S(1)} %get-tuple-element.26), channel_id=1, source_target_pairs={{0,130},{64,194},{128,0},{192,64},{2,128},{66,192},{130,2},{194,66... | collective-permute-start | bytes 393224 | tf_op jit(solution)/shard_map/ppermute | solution.py:250
  30.6 13.4 %collective-permute-start.3 = (bf16[2,128,512]{2,1,0:T(8,128)(2,1)}, bf16[2,128,512]{2,1,0:T(8,128)(2,1)}, u32[]{:S(2)}, u32[]{:S(2)}) collective-permute-start(bf16[2,128,512]{2,1,0:T(8,128)(2,1)} %collective-permute-done.1.refs_2_), channel_id=1, source_target_pairs={{0,64},{64,128},{128,192},{1,65},{65,129},{129,193},{2,66},{66,130... | collective-permute-start | bytes 786440 | tf_op jit(solution)/shard_map/ppermute | solution.py:274
  39.5 31.8 %copy-start.1 = (bf16[2,3,256,256]{3,2,1,0:T(8,128)(2,1)}, bf16[2,3,256,256]{3,2,1,0:T(8,128)(2,1)S(1)}, u32[]{:S(2)}) copy-start(bf16[2,3,256,256]{3,2,1,0:T(8,128)(2,1)S(1)} %pad_maximum_fusion.1.refs_0_) | copy-start | bytes 2359300
  39.5 31.8 %collective-permute-start.16 = (bf16[2,3,256,256]{3,2,1,0:T(8,128)(2,1)S(1)}, bf16[2,3,256,256]{3,2,1,0:T(8,128)(2,1)}, u32[]{:S(2)}, u32[]{:S(2)}) collective-permute-start(bf16[2,3,256,256]{3,2,1,0:T(8,128)(2,1)S(1)} %pad_maximum_fusion.1.refs_0_), channel_id=1, source_target_pairs={{0,12},{2,14},{4,0},{6,2},{8,4},{10,6},{12,8},{14,10},{16,28},{18,... | collective-permute-start | bytes 2359304 | tf_op jit(solution)/shard_map/ppermute | solution.py:256
  43.0 23.0 %collective-permute-start.18 = (bf16[3,256,256]{2,1,0:T(8,128)(2,1)}, bf16[3,256,256]{2,1,0:T(8,128)(2,1)}, u32[]{:S(2)}, u32[]{:S(2)}) collective-permute-start(bf16[3,256,256]{2,1,0:T(8,128)(2,1)} %get-tuple-element.31), channel_id=1, source_target_pairs={{0,4},{2,6},{4,0},{6,2},{8,12},{10,14},{12,8},{14,10},{16,20},{18,... | collective-permute-start | bytes 1179656 | tf_op jit(solution)/shard_map/ppermute | solution.py:254
  43.1 8.3 %collective-permute-start = (bf16[2,128,512]{2,1,0:T(8,128)(2,1)S(1)}, bf16[2,128,512]{2,1,0:T(8,128)(2,1)}, u32[]{:S(2)}, u32[]{:S(2)}) collective-permute-start(bf16[2,128,512]{2,1,0:T(8,128)(2,1)S(1)} %copy-done.3), channel_id=1, source_target_pairs={{0,1},{1,0},{2,3},{3,2},{4,5},{5,4},{6,7},{7,6},{8,9},{9,8},{10,11... | collective-permute-start | bytes 786440 | tf_op jit(solution)/shard_map/ppermute | solution.py:275
  44.0 22.0 %collective-permute-start.5 = (bf16[2,128,512]{2,1,0:T(8,128)(2,1)}, bf16[2,128,512]{2,1,0:T(8,128)(2,1)S(1)}, u32[]{:S(2)}, u32[]{:S(2)}) collective-permute-start(bf16[2,128,512]{2,1,0:T(8,128)(2,1)} %collective-permute-done.3.refs_4_), channel_id=1, source_target_pairs={{0,64},{64,128},{128,192},{1,65},{65,129},{129,193},{2,66},{66,130... | collective-permute-start | bytes 786440 | tf_op jit(solution)/shard_map/ppermute | solution.py:274
  48.2 26.1 %collective-permute-start.8 = (bf16[16,128,128]{2,1,0:T(8,128)(2,1)}, bf16[16,128,128]{2,1,0:T(8,128)(2,1)S(1)}, u32[]{:S(2)}, u32[]{:S(2)}) collective-permute-start(bf16[16,128,128]{2,1,0:T(8,128)(2,1)} %get-tuple-element.16), channel_id=1, source_target_pairs={{0,2},{2,0},{4,6},{6,4},{8,10},{10,8},{12,14},{14,12},{16,18},{18,... | collective-permute-start | bytes 1572872 | tf_op jit(solution)/shard_map/ppermute | solution.py:299
  51.3 16.9 %collective-permute-start.2 = (bf16[2,128,512]{2,1,0:T(8,128)(2,1)}, bf16[2,128,512]{2,1,0:T(8,128)(2,1)S(1)}, u32[]{:S(2)}, u32[]{:S(2)}) collective-permute-start(bf16[2,128,512]{2,1,0:T(8,128)(2,1)} %collective-permute-done.1.refs_2_), channel_id=1, source_target_pairs={{0,1},{1,0},{2,3},{3,2},{4,5},{5,4},{6,7},{7,6},{8,9},{9,8},{10,11... | collective-permute-start | bytes 786440 | tf_op jit(solution)/shard_map/ppermute | solution.py:275
  66.0 5.2 %collective-permute-start.4 = (bf16[2,128,512]{2,1,0:T(8,128)(2,1)}, bf16[2,128,512]{2,1,0:T(8,128)(2,1)}, u32[]{:S(2)}, u32[]{:S(2)}) collective-permute-start(bf16[2,128,512]{2,1,0:T(8,128)(2,1)} %collective-permute-done.3.refs_4_), channel_id=1, source_target_pairs={{0,1},{1,0},{2,3},{3,2},{4,5},{5,4},{6,7},{7,6},{8,9},{9,8},{10,11... | collective-permute-start | bytes 786440 | tf_op jit(solution)/shard_map/ppermute | solution.py:275
  66.0 8.8 %copy-start.7 = (bf16[2,128,512]{2,1,0:T(8,128)(2,1)}, bf16[2,128,512]{2,1,0:T(8,128)(2,1)S(1)}, u32[]{:S(2)}) copy-start(bf16[2,128,512]{2,1,0:T(8,128)(2,1)S(1)} %collective-permute-done.5.refs_6_) | copy-start | bytes 786436
  66.0 5.3 %collective-permute-start.6 = (bf16[2,128,512]{2,1,0:T(8,128)(2,1)S(1)}, bf16[2,128,512]{2,1,0:T(8,128)(2,1)}, u32[]{:S(2)}, u32[]{:S(2)}) collective-permute-start(bf16[2,128,512]{2,1,0:T(8,128)(2,1)S(1)} %collective-permute-done.5.refs_6_), channel_id=1, source_target_pairs={{0,1},{1,0},{2,3},{3,2},{4,5},{5,4},{6,7},{7,6},{8,9},{9,8},{10,11... | collective-permute-start | bytes 786440 | tf_op jit(solution)/shard_map/ppermute | solution.py:275
  68.2 16.5 %copy-start.2 = (bf16[2,3,256,256]{3,2,1,0:T(8,128)(2,1)}, bf16[2,3,256,256]{3,2,1,0:T(8,128)(2,1)S(1)}, u32[]{:S(2)}) copy-start(bf16[2,3,256,256]{3,2,1,0:T(8,128)(2,1)S(1)} %pad_maximum_fusion.2.refs_4_) | copy-start | bytes 2359300
  68.2 6.7 %copy-start.8 = (bf16[2,128,512]{2,1,0:T(8,128)(2,1)}, bf16[2,128,512]{2,1,0:T(8,128)(2,1)S(1)}, u32[]{:S(2)}) copy-start(bf16[2,128,512]{2,1,0:T(8,128)(2,1)S(1)} %collective-permute-done.2.refs_3_) | copy-start | bytes 786436
  68.2 22.2 %collective-permute-start.15 = (bf16[2,3,256,256]{3,2,1,0:T(8,128)(2,1)S(1)}, bf16[2,3,256,256]{3,2,1,0:T(8,128)(2,1)}, u32[]{:S(2)}, u32[]{:S(2)}) collective-permute-start(bf16[2,3,256,256]{3,2,1,0:T(8,128)(2,1)S(1)} %pad_maximum_fusion.1.refs_0_), channel_id=1, source_target_pairs={{0,8},{2,10},{4,12},{6,14},{8,0},{10,2},{12,4},{14,6},{16,24},{18,... | collective-permute-start | bytes 2359304 | tf_op jit(solution)/shard_map/ppermute | solution.py:256
  71.2 35.0 %collective-permute-start.14 = (bf16[2,3,256,256]{3,2,1,0:T(8,128)(2,1)S(1)}, bf16[2,3,256,256]{3,2,1,0:T(8,128)(2,1)}, u32[]{:S(2)}, u32[]{:S(2)}) collective-permute-start(bf16[2,3,256,256]{3,2,1,0:T(8,128)(2,1)S(1)} %pad_maximum_fusion.1.refs_0_), channel_id=1, source_target_pairs={{0,4},{2,6},{4,8},{6,10},{8,12},{10,14},{12,0},{14,2},{16,20},{18,... | collective-permute-start | bytes 2359304 | tf_op jit(solution)/shard_map/ppermute | solution.py:256
  71.3 36.1 %collective-permute-start.21 = (bf16[2,3,256,256]{3,2,1,0:T(8,128)(2,1)S(1)}, bf16[2,3,256,256]{3,2,1,0:T(8,128)(2,1)}, u32[]{:S(2)}, u32[]{:S(2)}) collective-permute-start(bf16[2,3,256,256]{3,2,1,0:T(8,128)(2,1)S(1)} %pad_maximum_fusion.2.refs_4_), channel_id=1, source_target_pairs={{0,48},{2,50},{4,52},{6,54},{8,56},{10,58},{12,60},{14,62},{16,0},... | collective-permute-start | bytes 2359304 | tf_op jit(solution)/shard_map/ppermute | solution.py:256
  71.4 36.0 %collective-permute-start.20 = (bf16[2,3,256,256]{3,2,1,0:T(8,128)(2,1)S(1)}, bf16[2,3,256,256]{3,2,1,0:T(8,128)(2,1)}, u32[]{:S(2)}, u32[]{:S(2)}) collective-permute-start(bf16[2,3,256,256]{3,2,1,0:T(8,128)(2,1)S(1)} %pad_maximum_fusion.2.refs_4_), channel_id=1, source_target_pairs={{0,32},{2,34},{4,36},{6,38},{8,40},{10,42},{12,44},{14,46},{16,48}... | collective-permute-start | bytes 2359304 | tf_op jit(solution)/shard_map/ppermute | solution.py:256
  74.3 34.9 %collective-permute-start.19 = (bf16[2,3,256,256]{3,2,1,0:T(8,128)(2,1)S(1)}, bf16[2,3,256,256]{3,2,1,0:T(8,128)(2,1)}, u32[]{:S(2)}, u32[]{:S(2)}) collective-permute-start(bf16[2,3,256,256]{3,2,1,0:T(8,128)(2,1)S(1)} %pad_maximum_fusion.2.refs_4_), channel_id=1, source_target_pairs={{0,16},{2,18},{4,20},{6,22},{8,24},{10,26},{12,28},{14,30},{16,32}... | collective-permute-start | bytes 2359304 | tf_op jit(solution)/shard_map/ppermute | solution.py:256
  90.3 18.8 %collective-permute-start.9 = (bf16[2,4,2,128,128]{4,3,2,1,0:T(8,128)(2,1)S(1)}, bf16[2,4,2,128,128]{4,3,2,1,0:T(8,128)(2,1)S(1)}, u32[]{:S(2)}, u32[]{:S(2)}) collective-permute-start(bf16[2,4,2,128,128]{4,3,2,1,0:T(8,128)(2,1)S(1)} %fusion.1), channel_id=1, source_target_pairs={{0,1},{1,0},{2,3},{3,2},{4,5},{5,4},{6,7},{7,6},{8,9},{9,8},{10,11... | collective-permute-start | bytes 1572872 | tf_op jit(solution)/shard_map/ppermute | solution.py:302
  106.3 2.9 %collective-permute-start.7 = (bf16[128,2048]{1,0:T(8,128)(2,1)}, bf16[128,2048]{1,0:T(8,128)(2,1)S(1)}, u32[]{:S(2)}, u32[]{:S(2)}) collective-permute-start(bf16[128,2048]{1,0:T(8,128)(2,1)} %get-tuple-element.15.mine), channel_id=1, source_target_pairs={{0,1},{1,0},{2,3},{3,2},{4,5},{5,4},{6,7},{7,6},{8,9},{9,8},{10,11... | collective-permute-start | bytes 1572872 | tf_op jit(solution)/shard_map/ppermute | solution.py:305
  109.2 0.8 copy-start.4
  110.0 0.8 copy-start.5
  121.4 2.2 %collective-permute-start.22 = (bf16[128,2048]{1,0:T(8,128)(2,1)}, bf16[128,2048]{1,0:T(8,128)(2,1)S(1)}, u32[]{:S(2)}, u32[]{:S(2)}) collective-permute-start(bf16[128,2048]{1,0:T(8,128)(2,1)} %get-tuple-element.18), channel_id=1, source_target_pairs={{0,1},{1,0},{2,3},{3,2},{4,5},{5,4},{6,7},{7,6},{8,9},{9,8},{10,11... | collective-permute-start | bytes 1572872 | tf_op jit(solution)/shard_map/ppermute | solution.py:307
  123.6 0.8 copy-start.6
  132.6 7.0 %copy-start = (bf16[4,2,128,512]{3,2,1,0:T(8,128)(2,1)S(1)}, bf16[4,2,128,512]{3,2,1,0:T(8,128)(2,1)}, u32[]{:S(2)}) copy-start(bf16[4,2,128,512]{3,2,1,0:T(8,128)(2,1)} %get-tuple-element.21) | copy-start | bytes 3145732
  132.6 3.0 %collective-permute-start.23 = (bf16[4,2,128,512]{3,2,1,0:T(8,128)(2,1)}, bf16[4,2,128,512]{3,2,1,0:T(8,128)(2,1)S(1)}, u32[]{:S(2)}, u32[]{:S(2)}) collective-permute-start(bf16[4,2,128,512]{3,2,1,0:T(8,128)(2,1)} %get-tuple-element.22), channel_id=1, source_target_pairs={{0,1},{1,0},{2,3},{3,2},{4,5},{5,4},{6,7},{7,6},{8,9},{9,8},{10,11... | collective-permute-start | bytes 3145736 | tf_op jit(solution)/shard_map/ppermute | solution.py:309
  136.9 2.7 %collective-permute-start.26 = (bf16[2,128,512]{2,1,0:T(8,128)(2,1)S(1)}, bf16[2,128,512]{2,1,0:T(8,128)(2,1)S(1)}, u32[]{:S(2)}, u32[]{:S(2)}) collective-permute-start(bf16[2,128,512]{2,1,0:T(8,128)(2,1)S(1)} %get-tuple-element.24), channel_id=1, source_target_pairs={{192,128},{193,129},{194,130},{195,131},{196,132},{197,133},{198,1... | collective-permute-start | bytes 786440 | tf_op jit(solution)/shard_map/ppermute | solution.py:312
  137.6 10.6 %collective-permute-start.24 = (bf16[2,128,512]{2,1,0:T(8,128)(2,1)S(1)}, bf16[2,128,512]{2,1,0:T(8,128)(2,1)S(1)}, u32[]{:S(2)}, u32[]{:S(2)}) collective-permute-start(bf16[2,128,512]{2,1,0:T(8,128)(2,1)S(1)} %get-tuple-element.23), channel_id=1, source_target_pairs={{64,0},{128,64},{192,128},{65,1},{129,65},{193,129},{66,2},{130,66... | collective-permute-start | bytes 786440 | tf_op jit(solution)/shard_map/ppermute | solution.py:313
  138.9 9.3 %collective-permute-start.25 = (bf16[2,128,512]{2,1,0:T(8,128)(2,1)S(1)}, bf16[2,128,512]{2,1,0:T(8,128)(2,1)S(1)}, u32[]{:S(2)}, u32[]{:S(2)}) collective-permute-start(bf16[2,128,512]{2,1,0:T(8,128)(2,1)S(1)} %get-tuple-element.25), channel_id=1, source_target_pairs={{192,64},{193,65},{194,66},{195,67},{196,68},{197,69},{198,70},{19... | collective-permute-start | bytes 786440 | tf_op jit(solution)/shard_map/ppermute | solution.py:314
  139.7 24.1 %collective-permute-start.27 = (bf16[2,128,512]{2,1,0:T(8,128)(2,1)S(1)}, bf16[2,128,512]{2,1,0:T(8,128)(2,1)S(1)}, u32[]{:S(2)}, u32[]{:S(2)}) collective-permute-start(bf16[2,128,512]{2,1,0:T(8,128)(2,1)S(1)} %fusion.2), channel_id=1, source_target_pairs={{128,0},{129,1},{130,2},{131,3},{132,4},{133,5},{134,6},{135,7},{1... | collective-permute-start | bytes 786440 | tf_op jit(solution)/shard_map/ppermute | solution.py:316
where the time goes:
time: 168 us; the launch traced here: 165 us
  waiting for transfers between devices  72.7 us (43%)
  starting transfers between devices  47.1 us (28%)
  Pallas kernels  30.3 us (18%)
  other arithmetic  8 us (5%)
  local copies, waits for them, and re-layouts  5.64 us (3%)
    ppermute x6, waiting for transfers between devices, spread_weights(): arrays += [slab] + [lax.ppermute(slab, 'tp', far(d)) for d in (1, 2, 3)]  23.3 us
    ppermute x2, waiting for transfers between devices, spread_weights(): other = lax.ppermute(slab, 'tp', pair)  18.4 us
    ppermute x1, waiting for transfers between devices, step(): joined = lax.ppermute(joined, 'grp', [(2, 0)])  15.6 us
    ppermute x3, starting transfers between devices, gather_keys(): piece = lax.ppermute(piece, 'grp', up(1))  13.5 us
    pallas_call x1, Pallas kernels, project(): pl.pallas_call(project_body, grid_spec=pltpu.PrefetchScalarGridSpec(num_s...  10.6 us
    pallas_call x1, Pallas kernels, forward(): pl.pallas_call(forward_body, grid_spec=pltpu.PrefetchScalarGridSpec(num_s...  9.84 us
    ppermute x6, starting transfers between devices, spread_weights(): arrays += [slab] + [lax.ppermute(slab, 'tp', far(d)) for d in (1, 2, 3)]  9.36 us
    pallas_call x1, Pallas kernels, backward(): pl.pallas_call(backward_body, grid=(KV_HEADS,), in_specs=[pl.BlockSpec((N...  8.17 us
  transfers between devices with their start and end apart: 29, of which 11 were waited for; matrix products, arithmetic and copies ran while one was open for 5% of the time, Pallas kernels for 7%

commit v1 on v0

--- a/solution.py
+++ b/solution.py
@@ -76,12 +76,22 @@
     return jnp.concatenate([rows[g * ROWS : (g + 1) * ROWS] for g in range(GROUP)], axis=1)
 
 
+def kv_lanes(h):
+    return pl.ds(pl.multiple_of(h * HD, HD), HD), pl.ds(pl.multiple_of(h * GROUP * HD, GROUP * HD), GROUP * HD)
+
+
+VMEM_SPEC = pl.BlockSpec(memory_space=pltpu.VMEM)
+HBM_SPEC = pl.BlockSpec(memory_space=pltpu.HBM)
+PARAMS = pltpu.CompilerParams(vmem_limit_bytes=32 * 2**20)
+
+
 def forward_body(info, q, *refs):
     pieces, (wide, low, probs) = refs[:SLOTS], refs[SLOTS:]
     grp, rep = info[0], info[1]
+    head, heads = kv_lanes(pl.program_id(0))
     q4 = stack_heads(q[...])
-    keys = jnp.concatenate([p[0] for p in pieces], axis=0)
-    values = jnp.concatenate([p[1] for p in pieces], axis=0)
+    keys = jnp.concatenate([p[0, :, head] for p in pieces], axis=0)
+    values = jnp.concatenate([p[1, :, head] for p in pieces], axis=0)
     scores = nt(q4, keys) * INV_ROOT
     row = lax.broadcasted_iota(jnp.int32, (GROUP * ROWS, ROWS), 0) % ROWS
     col = lax.broadcasted_iota(jnp.int32, (GROUP * ROWS, ROWS), 1)
@@ -103,7 +113,7 @@
     probs[...] = prob_low
     out = spread_heads(nn(prob_low, values))
     wide[...] = out
-    low[...] = out.astype(jnp.bfloat16)
+    low[:, heads] = out.astype(jnp.bfloat16)
 
 
 def forward(info, q, pieces):
@@ -113,18 +123,19 @@
             num_scalar_prefetch=1,
             grid=(KV_HEADS,),
             in_specs=[pl.BlockSpec((ROWS, GROUP * HD), lambda h, i: (0, h))]
-            + [pl.BlockSpec((2, ROWS, HD), lambda h, i: (0, 0, h))] * SLOTS,
+            + [VMEM_SPEC] * SLOTS,
             out_specs=[
                 pl.BlockSpec((ROWS, GROUP * HD), lambda h, i: (0, h)),
-                pl.BlockSpec((ROWS, GROUP * HD), lambda h, i: (0, h)),
+                VMEM_SPEC,
                 pl.BlockSpec((None, GROUP * ROWS, SLOTS * ROWS), lambda h, i: (h, 0, 0)),
             ],
         ),
         out_shape=[
             jax.ShapeDtypeStruct((ROWS, FEAT), jnp.float32),
-            jax.ShapeDtypeStruct((ROWS, FEAT), jnp.bfloat16),
+            pltpu.VMEM((ROWS, FEAT), jnp.bfloat16),
             jax.ShapeDtypeStruct((KV_HEADS, GROUP * ROWS, SLOTS * ROWS), jnp.bfloat16),
         ],
+        compiler_params=PARAMS,
         cost_estimate=pl.CostEstimate(flops=10**10, bytes_accessed=8 * 10**6, transcendentals=2 * 10**6),
         name="attn_fwd",
     )(info, q, *pieces)
@@ -192,10 +203,8 @@
                 pltpu.SemaphoreType.DMA((17,)),
             ],
         ),
-        out_shape=[
-            jax.ShapeDtypeStruct((ROWS, FEAT), jnp.float32),
-            jax.ShapeDtypeStruct((ROWS, FEAT), jnp.bfloat16),
-        ],
+        out_shape=[pltpu.VMEM((ROWS, FEAT), jnp.float32), pltpu.VMEM((ROWS, FEAT), jnp.bfloat16)],
+        compiler_params=PARAMS,
         cost_estimate=pl.CostEstimate(flops=10**10, bytes_accessed=12 * 10**6, transcendentals=0),
         name="project",
     )(info, mine, theirs, target_mine, target_theirs, own, *arrays)
@@ -203,12 +212,13 @@
 
 def backward_body(probs, part, got, wide, q, *refs):
     pieces, (grad_q, terms_mine, terms_theirs) = refs[:SLOTS], refs[SLOTS:]
-    grad = (part[...] + got[...].astype(jnp.float32)).astype(jnp.bfloat16)
+    head, heads = kv_lanes(pl.program_id(0))
+    grad = (part[:, heads] + got[:, heads].astype(jnp.float32)).astype(jnp.bfloat16)
     delta = stack_heads(grad.astype(jnp.float32) * wide[...]).sum(axis=1, keepdims=True)
     g4 = stack_heads(grad)
     q4 = stack_heads(q[...])
-    keys = jnp.concatenate([p[0] for p in pieces], axis=0)
-    values = jnp.concatenate([p[1] for p in pieces], axis=0)
+    keys = jnp.concatenate([p[0, :, head] for p in pieces], axis=0)
+    values = jnp.concatenate([p[1, :, head] for p in pieces], axis=0)
     p_low = probs[...]
     grad_prob = nt(g4, values)
     grad_score = (p_low.astype(jnp.float32) * (grad_prob - delta) * INV_ROOT).astype(jnp.bfloat16)
@@ -217,24 +227,25 @@
     value_terms = tn(p_low, g4).astype(jnp.bfloat16)
     for s in range(SLOTS):
         out = terms_theirs if s % 2 else terms_mine
-        out[s // 2, 0] = key_terms[s * ROWS : (s + 1) * ROWS]
-        out[s // 2, 1] = value_terms[s * ROWS : (s + 1) * ROWS]
+        out[s // 2, 0, :, head] = key_terms[s * ROWS : (s + 1) * ROWS]
+        out[s // 2, 1, :, head] = value_terms[s * ROWS : (s + 1) * ROWS]
 
 
 def backward(probs, part, got, wide, q, pieces):
     rows = pl.BlockSpec((ROWS, GROUP * HD), lambda h: (0, h))
-    terms = pl.BlockSpec((N_GRP, 2, ROWS, HD), lambda h: (0, 0, 0, h))
+    terms = pltpu.VMEM((N_GRP, 2, ROWS, KV_HEADS * HD), jnp.bfloat16)
     return pl.pallas_call(
         backward_body,
         grid=(KV_HEADS,),
-        in_specs=[pl.BlockSpec((None, GROUP * ROWS, SLOTS * ROWS), lambda h: (h, 0, 0)), rows, rows, rows, rows]
-        + [pl.BlockSpec((2, ROWS, HD), lambda h: (0, 0, h))] * SLOTS,
-        out_specs=[rows, terms, terms],
+        in_specs=[pl.BlockSpec((None, GROUP * ROWS, SLOTS * ROWS), lambda h: (h, 0, 0)), VMEM_SPEC, VMEM_SPEC, rows, rows]
+        + [VMEM_SPEC] * SLOTS,
+        out_specs=[rows, VMEM_SPEC, VMEM_SPEC],
         out_shape=[
             jax.ShapeDtypeStruct((ROWS, FEAT), jnp.bfloat16),
-            jax.ShapeDtypeStruct((N_GRP, 2, ROWS, KV_HEADS * HD), jnp.bfloat16),
-            jax.ShapeDtypeStruct((N_GRP, 2, ROWS, KV_HEADS * HD), jnp.bfloat16),
+            terms,
+            terms,
         ],
+        compiler_params=PARAMS,
         cost_estimate=pl.CostEstimate(flops=10**10, bytes_accessed=8 * 10**6, transcendentals=0),
         name="attn_bwd",
     )(probs, part, got, wide, q, *pieces)
@@ -301,10 +312,15 @@
     give = lax.dynamic_index_in_dim(target_mine, 1 - rep, 2, keepdims=False)
     target_theirs = lax.ppermute(give, "rep", SWAP)
 
+    pieces = [pltpu.with_memory_space_constraint(a, pltpu.VMEM) for a in pieces]
     wide, low, probs = forward(info, query, pieces)
     theirs = lax.ppermute(low, "rep", SWAP)
+    theirs, target_mine, target_theirs = [
+        pltpu.with_memory_space_constraint(a, pltpu.VMEM) for a in (theirs, target_mine, target_theirs)
+    ]
     part, give = project(info, low, theirs, target_mine, target_theirs, projection, arrays)
     got = lax.ppermute(give, "rep", SWAP)
+    got = pltpu.with_memory_space_constraint(got, pltpu.VMEM)
     grad_q, terms_mine, terms_theirs = backward(probs, part, got, wide, query, pieces)
     got = lax.ppermute(terms_theirs, "rep", SWAP)
     terms = [terms_mine[d].astype(jnp.float32) + got[d].astype(jnp.float32) for d in range(N_GRP)]

time: 168 us -> 159 us (0.946)
  Pallas kernels: 30.3 us -> 23.7 us
    pallas_call x1, Pallas kernels: 10.6 us -> 6.41 us  [project(): pl.pallas_call(project_body, grid_spec=pltpu.PrefetchScalarGridSpec(num_s...]
    unnamed x18 -> x8, local copies, waits for them, and re-layouts: 2.43 us -> 0.02 us
  transfers between devices with their start and end apart: 29 -> 29, of which waited for: 11 -> 11; matrix products, arithmetic and copies ran while one was open for 5% -> 7% of each run, Pallas kernels for 7% -> 7%
where the time goes in v1:
time: 159 us; the launch traced here: 156 us
  waiting for transfers between devices  72.6 us (46%)
  starting transfers between devices  46.2 us (29%)
  Pallas kernels  23.7 us (15%)
  other arithmetic  8.34 us (5%)
  local copies, waits for them, and re-layouts  4.18 us (3%)
    ppermute x6, waiting for transfers between devices, spread_weights(): arrays += [slab] + [lax.ppermute(slab, 'tp', far(d)) for d in (1, 2, 3)]  23.1 us
    ppermute x2, waiting for transfers between devices, spread_weights(): other = lax.ppermute(slab, 'tp', pair)  17.5 us
    ppermute x1, waiting for transfers between devices, step(): joined = lax.ppermute(joined, 'grp', [(2, 0)])  17.1 us
    ppermute x3, starting transfers between devices, gather_keys(): piece = lax.ppermute(piece, 'grp', up(1))  12 us
    ppermute x6, starting transfers between devices, spread_weights(): arrays += [slab] + [lax.ppermute(slab, 'tp', far(d)) for d in (1, 2, 3)]  9.36 us
    pallas_call x1, Pallas kernels, forward(): pl.pallas_call(forward_body, grid_spec=pltpu.PrefetchScalarGridSpec(num_s...  8.69 us
    all_to_all x1, starting transfers between devices, step(): lax.all_to_all(rows, 'tp', split_axis=0, concat_axis=0, tiled=True, axis_...  7.45 us
    ppermute x1, waiting for transfers between devices, step(): near = lax.ppermute(low_terms[1], 'grp', down(1))  7.11 us
  transfers between devices with their start and end apart: 29, of which 11 were waited for; matrix products, arithmetic and copies ran while one was open for 7% of the time, Pallas kernels for 7%

profile of v1, /device:TPU:4, one launch (start us, length us, event | category | flops | bytes accessed | tf_op | source)
XLA Modules:
  0.0 156.1 jit_solution(8154693638854992620)
XLA Ops:
  0.7 1.0 constant_dynamic-slice_fusion.2
  1.7 3.3 %collective-permute-start.12 = (bf16[256,256]{1,0:T(8,128)(2,1)S(1)}, bf16[256,256]{1,0:T(8,128)(2,1)S(1)}, u32[]{:S(2)}, u32[]{:S(2)}) collective-permute-start(bf16[256,256]{1,0:T(8,128)(2,1)S(1)} %get-tuple-element.27), channel_id=1, source_target_pairs={{0,128},{64,192},{128,2},{192,66},{2,130},{66,194},{130,0},{194,64... | collective-permute-start | bytes 393224 | tf_op jit(solution)/shard_map/ppermute | solution.py:261
  5.1 2.7 %collective-permute-start.11 = (bf16[2,256,256]{2,1,0:T(8,128)(2,1)S(1)}, bf16[2,256,256]{2,1,0:T(8,128)(2,1)S(1)}, u32[]{:S(2)}, u32[]{:S(2)}) collective-permute-start(bf16[2,256,256]{2,1,0:T(8,128)(2,1)S(1)} %pad_maximum_fusion.5), channel_id=1, source_target_pairs={{0,194},{64,0},{128,64},{192,128},{2,192},{66,2},{130,66},{194,130... | collective-permute-start | bytes 786440 | tf_op jit(solution)/shard_map/ppermute | solution.py:260
  7.8 0.0 collective-permute-start.10
  7.8 0.7 bitcast_convert_fusion.1
  8.5 2.5 %multiply_convert_fusion = bf16[32,128,128]{2,1,0:T(8,128)(2,1)} fusion(bf16[32,128,128]{2,1,0:T(8,128)(2,1)} %param.9, f32[32,128]{1,0:T(8,128)S(1)} %bitcast_convert_fusion.1), kind=kLoop, calls=%fused_computation | loop fusion | flops 1572864 | bytes 2113536 | tf_op jit(solution)/shard_map/convert_element_type | solution.py:297
  11.0 7.5 %all-to-all-start = ((bf16[16,2,128,128]{3,2,1,0:T(8,128)(2,1)}), bf16[16,2,128,128]{3,2,1,0:T(8,128)(2,1)}, u32[]{:S(2)}, u32[]{:S(2)}) async-start(bf16[16,2,128,128]{3,2,1,0:T(8,128)(2,1)} %bitcast.7), calls=%async_computation | async-start | bytes 2097152 | tf_op jit(solution)/shard_map/all_to_all | solution.py:299
  18.5 1.1 collective-permute-done.10
  19.6 0.0 collective-permute-done.12
  19.6 0.1 fusion.9
  19.7 1.3 collective-permute-start.13
  20.9 1.7 %join.1.refs_0_ = bf16[2,128,512]{2,1,0:T(8,128)(2,1)} custom-call(bf16[1,128,512]{2,1,0:T(8,128)(2,1)} %keys.1, bf16[1,128,512]{2,1,0:T(8,128)(2,1)} %values.1), custom_call_target="tpu_custom_call" | custom-call | tf_op jit(solution)/shard_map/join/pallas_call | solution.py:277
  22.6 3.5 %collective-permute-start.1 = (bf16[2,128,512]{2,1,0:T(8,128)(2,1)}, bf16[2,128,512]{2,1,0:T(8,128)(2,1)S(1)}, u32[]{:S(2)}, u32[]{:S(2)}) collective-permute-start(bf16[2,128,512]{2,1,0:T(8,128)(2,1)} %join.1.refs_0_), channel_id=1, source_target_pairs={{0,64},{64,128},{128,192},{1,65},{65,129},{129,193},{2,66},{66,130... | collective-permute-start | bytes 786440 | tf_op jit(solution)/shard_map/ppermute | solution.py:285
  26.1 2.2 %collective-permute-start.17 = (bf16[256,256]{1,0:T(8,128)(2,1)S(1)}, bf16[256,256]{1,0:T(8,128)(2,1)S(1)}, u32[]{:S(2)}, u32[]{:S(2)}) collective-permute-start(bf16[256,256]{1,0:T(8,128)(2,1)S(1)} %get-tuple-element.26), channel_id=1, source_target_pairs={{0,130},{64,194},{128,0},{192,64},{2,128},{66,192},{130,2},{194,66... | collective-permute-start | bytes 393224 | tf_op jit(solution)/shard_map/ppermute | solution.py:261
  28.4 2.2 %collective-permute-done.1.refs_2_ = bf16[2,128,512]{2,1,0:T(8,128)(2,1)S(1)} collective-permute-done((bf16[2,128,512]{2,1,0:T(8,128)(2,1)}, bf16[2,128,512]{2,1,0:T(8,128)(2,1)S(1)}, u32[]{:S(2)}, u32[]{:S(2)}) %collective-permute-start.1) | collective-permute-done | bytes 262176 | tf_op jit(solution)/shard_map/ppermute | solution.py:285
  30.6 4.3 %collective-permute-start.3 = (bf16[2,128,512]{2,1,0:T(8,128)(2,1)S(1)}, bf16[2,128,512]{2,1,0:T(8,128)(2,1)S(1)}, u32[]{:S(2)}, u32[]{:S(2)}) collective-permute-start(bf16[2,128,512]{2,1,0:T(8,128)(2,1)S(1)} %collective-permute-done.1.refs_2_), channel_id=1, source_target_pairs={{0,64},{64,128},{128,192},{1,65},{65,129},{129,193},{2,66},{66,130... | collective-permute-start | bytes 786440 | tf_op jit(solution)/shard_map/ppermute | solution.py:285
  34.9 4.5 %collective-permute-done.13 = bf16[3,256,256]{2,1,0:T(8,128)(2,1)S(1)} collective-permute-done((bf16[3,256,256]{2,1,0:T(8,128)(2,1)S(1)}, bf16[3,256,256]{2,1,0:T(8,128)(2,1)S(1)}, u32[]{:S(2)}, u32[]{:S(2)}) %collective-permute-start.13) | collective-permute-done | bytes 393248 | tf_op jit(solution)/shard_map/ppermute | solution.py:265
  39.4 0.1 pad_maximum_fusion.1.refs_0_
  39.5 2.8 %collective-permute-start.16 = (bf16[2,3,256,256]{3,2,1,0:T(8,128)(2,1)S(1)}, bf16[2,3,256,256]{3,2,1,0:T(8,128)(2,1)S(1)}, u32[]{:S(2)}, u32[]{:S(2)}) collective-permute-start(bf16[2,3,256,256]{3,2,1,0:T(8,128)(2,1)S(1)} %pad_maximum_fusion.1.refs_0_), channel_id=1, source_target_pairs={{0,12},{2,14},{4,0},{6,2},{8,4},{10,6},{12,8},{14,10},{16,28},{18,... | collective-permute-start | bytes 2359304 | tf_op jit(solution)/shard_map/ppermute | solution.py:267
  42.2 1.0 fusion.8
  43.2 0.0 collective-permute-start.18
  43.2 0.1 collective-permute-start
  43.3 0.0 all-to-all-done
  43.3 2.3 %constant_dynamic-slice_fusion.1 = (bf16[16,1,128,128]{3,2,1,0:T(8,128)(2,1)}, bf16[16,128,128]{2,1,0:T(8,128)(2,1)}) fusion(bf16[16,2,128,128]{3,2,1,0:T(8,128)(2,1)} %all-to-all-done, s32[]{:T(128)S(6)} %select_n.48, s32[]{:T(128)S(6)} %select_n.47), kind=kLoop, calls=%fused_computation.26 | loop fusion | bytes 2097160 | tf_op jit(solution)/shard_map/jit(dynamic_index_in_dim)/dynamic_slice | solution.py:307
  45.7 0.0 collective-permute-done.3.refs_4_
  45.7 4.2 %collective-permute-start.5 = (bf16[2,128,512]{2,1,0:T(8,128)(2,1)S(1)}, bf16[2,128,512]{2,1,0:T(8,128)(2,1)S(1)}, u32[]{:S(2)}, u32[]{:S(2)}) collective-permute-start(bf16[2,128,512]{2,1,0:T(8,128)(2,1)S(1)} %collective-permute-done.3.refs_4_), channel_id=1, source_target_pairs={{0,64},{64,128},{128,192},{1,65},{65,129},{129,193},{2,66},{66,130... | collective-permute-start | bytes 786440 | tf_op jit(solution)/shard_map/ppermute | solution.py:285
  49.9 3.1 %collective-permute-start.8 = (bf16[16,128,128]{2,1,0:T(8,128)(2,1)}, bf16[16,128,128]{2,1,0:T(8,128)(2,1)}, u32[]{:S(2)}, u32[]{:S(2)}) collective-permute-start(bf16[16,128,128]{2,1,0:T(8,128)(2,1)} %get-tuple-element.16), channel_id=1, source_target_pairs={{0,2},{2,0},{4,6},{6,4},{8,10},{10,8},{12,14},{14,12},{16,18},{18,... | collective-permute-start | bytes 1572872 | tf_op jit(solution)/shard_map/ppermute | solution.py:310
  53.0 0.0 collective-permute-done.refs_1_
  53.0 13.0 %collective-permute-done.18 = bf16[3,256,256]{2,1,0:T(8,128)(2,1)} collective-permute-done((bf16[3,256,256]{2,1,0:T(8,128)(2,1)}, bf16[3,256,256]{2,1,0:T(8,128)(2,1)}, u32[]{:S(2)}, u32[]{:S(2)}) %collective-permute-start.18) | collective-permute-done | bytes 393248 | tf_op jit(solution)/shard_map/ppermute | solution.py:265
  66.0 0.5 collective-permute-start.6
  66.5 0.1 stack.74.info
  66.6 1.2 pad_maximum_fusion.2.refs_4_
  67.8 0.0 collective-permute-done.2.refs_3_
  67.8 3.1 %collective-permute-start.15 = (bf16[2,3,256,256]{3,2,1,0:T(8,128)(2,1)S(1)}, bf16[2,3,256,256]{3,2,1,0:T(8,128)(2,1)S(1)}, u32[]{:S(2)}, u32[]{:S(2)}) collective-permute-start(bf16[2,3,256,256]{3,2,1,0:T(8,128)(2,1)S(1)} %pad_maximum_fusion.1.refs_0_), channel_id=1, source_target_pairs={{0,8},{2,10},{4,12},{6,14},{8,0},{10,2},{12,4},{14,6},{16,24},{18,... | collective-permute-start | bytes 2359304 | tf_op jit(solution)/shard_map/ppermute | solution.py:267
  70.8 0.0 collective-permute-done.16.refs_3_
  70.8 0.1 collective-permute-start.21
  71.0 2.9 %collective-permute-start.20 = (bf16[2,3,256,256]{3,2,1,0:T(8,128)(2,1)S(1)}, bf16[2,3,256,256]{3,2,1,0:T(8,128)(2,1)S(1)}, u32[]{:S(2)}, u32[]{:S(2)}) collective-permute-start(bf16[2,3,256,256]{3,2,1,0:T(8,128)(2,1)S(1)} %pad_maximum_fusion.2.refs_4_), channel_id=1, source_target_pairs={{0,32},{2,34},{4,36},{6,38},{8,40},{10,42},{12,44},{14,46},{16,48}... | collective-permute-start | bytes 2359304 | tf_op jit(solution)/shard_map/ppermute | solution.py:267
  73.8 0.0 collective-permute-done.8
  73.8 0.6 collective-permute-start.19
  74.4 8.7 %attn_fwd.1 = (f32[128,2048]{1,0:T(8,128)S(1)}, bf16[128,2048]{1,0:T(8,128)(2,1)S(1)}, bf16[4,512,1024]{2,1,0:T(8,128)(2,1)S(1)}) custom-call(s32[5]{0:T(128)S(1)} %stack.74.info, bf16[128,2048]{1,0:T(8,128)(2,1)S(1)} %bitcast.44, bf16[2,128,512]{2,1,0:T(8,128)(2,1)S(1)} %copy-done, bf16[2,128,512]{2,1,0:T(8,128)(2,1)S(1)} %collective-permute-done.refs_1_, ...), custom_call_target="tpu_custom_call" | custom-call | flops 10000000000 | bytes 8000000 | tf_op jit(solution)/shard_map/attn_fwd/pallas_call | solution.py:120
  83.1 0.0 copy-start.1
  83.2 1.2 fusion.1
  84.3 5.5 %collective-permute-done.15.refs_2_ = bf16[2,3,256,256]{3,2,1,0:T(8,128)(2,1)S(1)} collective-permute-done((bf16[2,3,256,256]{3,2,1,0:T(8,128)(2,1)S(1)}, bf16[2,3,256,256]{3,2,1,0:T(8,128)(2,1)S(1)}, u32[]{:S(2)}, u32[]{:S(2)}) %collective-permute-start.15) | collective-permute-done | bytes 786464 | tf_op jit(solution)/shard_map/ppermute | solution.py:267
  89.8 0.0 collective-permute-start.9
  89.8 15.8 %collective-permute-done.14.refs_1_ = bf16[2,3,256,256]{3,2,1,0:T(8,128)(2,1)S(1)} collective-permute-done((bf16[2,3,256,256]{3,2,1,0:T(8,128)(2,1)S(1)}, bf16[2,3,256,256]{3,2,1,0:T(8,128)(2,1)S(1)}, u32[]{:S(2)}, u32[]{:S(2)}) %collective-permute-start.14) | collective-permute-done | bytes 786464 | tf_op jit(solution)/shard_map/ppermute | solution.py:267
  105.7 0.0 collective-permute-start.7
  105.7 1.1 pad_maximum_fusion.target_mine
  106.9 1.7 %collective-permute-done.19.refs_5_ = bf16[2,3,256,256]{3,2,1,0:T(8,128)(2,1)S(1)} collective-permute-done((bf16[2,3,256,256]{3,2,1,0:T(8,128)(2,1)S(1)}, bf16[2,3,256,256]{3,2,1,0:T(8,128)(2,1)S(1)}, u32[]{:S(2)}, u32[]{:S(2)}) %collective-permute-start.19) | collective-permute-done | bytes 786464 | tf_op jit(solution)/shard_map/ppermute | solution.py:267
  108.6 6.4 %project.1 = (f32[128,2048]{1,0:T(8,128)S(1)}, bf16[128,2048]{1,0:T(8,128)(2,1)S(1)}) custom-call(s32[5]{0:T(128)S(1)} %stack.74.info, bf16[128,2048]{1,0:T(8,128)(2,1)S(1)} %get-tuple-element.15.mine, bf16[128,2048]{1,0:T(8,128)(2,1)S(1)} %collective-permute-done.7.theirs, bf16[2,4,2,2,128,128]{5,4,3,2,1,0:T(8,128)(2,1)S(1)} %pad_maximum_fusion.target_mine, ...), custom_call_target="tpu_custom_call" | custom-call | flops 10000000000 | bytes 12000000 | tf_op jit(solution)/shard_map/project/pallas_call | solution.py:192
  115.0 0.1 collective-permute-start.22
  115.1 1.9 %collective-permute-done.22.got = bf16[128,2048]{1,0:T(8,128)(2,1)S(1)} collective-permute-done((bf16[128,2048]{1,0:T(8,128)(2,1)S(1)}, bf16[128,2048]{1,0:T(8,128)(2,1)S(1)}, u32[]{:S(2)}, u32[]{:S(2)}) %collective-permute-start.22) | collective-permute-done | bytes 524320 | tf_op jit(solution)/shard_map/ppermute | solution.py:322
  117.0 7.0 %attn_bwd.1 = (bf16[128,2048]{1,0:T(8,128)(2,1)}, bf16[4,2,128,512]{3,2,1,0:T(8,128)(2,1)S(1)}, bf16[4,2,128,512]{3,2,1,0:T(8,128)(2,1)S(1)}) custom-call(bf16[4,512,1024]{2,1,0:T(8,128)(2,1)S(1)} %get-tuple-element.14.probs, f32[128,2048]{1,0:T(8,128)S(1)} %get-tuple-element.17.part, bf16[128,2048]{1,0:T(8,128)(2,1)S(1)} %collective-permute-done.22.got, ...), custom_call_target="tpu_custom_call" | custom-call | flops 10000000000 | bytes 8000000 | tf_op jit(solution)/shard_map/attn_bwd/pallas_call | solution.py:237
  123.9 0.1 collective-permute-start.23
  124.1 2.5 %collective-permute-done.23 = bf16[4,2,128,512]{3,2,1,0:T(8,128)(2,1)S(1)} collective-permute-done((bf16[4,2,128,512]{3,2,1,0:T(8,128)(2,1)S(1)}, bf16[4,2,128,512]{3,2,1,0:T(8,128)(2,1)S(1)}, u32[]{:S(2)}, u32[]{:S(2)}) %collective-permute-start.23) | collective-permute-done | bytes 1048608 | tf_op jit(solution)/shard_map/ppermute | solution.py:325
  126.6 0.2 fusion.6
  126.8 0.7 collective-permute-start.26
  127.5 1.3 collective-permute-start.24
  128.8 0.7 collective-permute-start.25
  129.5 0.1 fusion.2
  129.6 1.3 collective-permute-start.27
  130.9 7.1 %collective-permute-done.24 = bf16[2,128,512]{2,1,0:T(8,128)(2,1)S(1)} collective-permute-done((bf16[2,128,512]{2,1,0:T(8,128)(2,1)S(1)}, bf16[2,128,512]{2,1,0:T(8,128)(2,1)S(1)}, u32[]{:S(2)}, u32[]{:S(2)}) %collective-permute-start.24) | collective-permute-done | bytes 262176 | tf_op jit(solution)/shard_map/ppermute | solution.py:329
  138.0 17.1 %collective-permute-done.27 = bf16[2,128,512]{2,1,0:T(8,128)(2,1)S(1)} collective-permute-done((bf16[2,128,512]{2,1,0:T(8,128)(2,1)S(1)}, bf16[2,128,512]{2,1,0:T(8,128)(2,1)S(1)}, u32[]{:S(2)}, u32[]{:S(2)}) %collective-permute-start.27) | collective-permute-done | bytes 262176 | tf_op jit(solution)/shard_map/ppermute | solution.py:332
  155.2 0.2 fusion.5
  155.3 0.7 fusion.10
  (24 shorter events, 0.1 us)
Async XLA Ops:
  1.7 17.9 %collective-permute-start.12 = (bf16[256,256]{1,0:T(8,128)(2,1)S(1)}, bf16[256,256]{1,0:T(8,128)(2,1)S(1)}, u32[]{:S(2)}, u32[]{:S(2)}) collective-permute-start(bf16[256,256]{1,0:T(8,128)(2,1)S(1)} %get-tuple-element.27), channel_id=1, source_target_pairs={{0,128},{64,192},{128,2},{192,66},{2,130},{66,194},{130,0},{194,64... | collective-permute-start | bytes 393224 | tf_op jit(solution)/shard_map/ppermute | solution.py:261
  5.1 13.4 %collective-permute-start.11 = (bf16[2,256,256]{2,1,0:T(8,128)(2,1)S(1)}, bf16[2,256,256]{2,1,0:T(8,128)(2,1)S(1)}, u32[]{:S(2)}, u32[]{:S(2)}) collective-permute-start(bf16[2,256,256]{2,1,0:T(8,128)(2,1)S(1)} %pad_maximum_fusion.5), channel_id=1, source_target_pairs={{0,194},{64,0},{128,64},{192,128},{2,192},{66,2},{130,66},{194,130... | collective-permute-start | bytes 786440 | tf_op jit(solution)/shard_map/ppermute | solution.py:260
  7.8 11.8 %collective-permute-start.10 = (bf16[2,256,256]{2,1,0:T(8,128)(2,1)S(1)}, bf16[2,256,256]{2,1,0:T(8,128)(2,1)S(1)}, u32[]{:S(2)}, u32[]{:S(2)}) collective-permute-start(bf16[2,256,256]{2,1,0:T(8,128)(2,1)S(1)} %pad_maximum_fusion.5), channel_id=1, source_target_pairs={{0,64},{64,128},{128,192},{192,2},{2,66},{66,130},{130,194},{194,0... | collective-permute-start | bytes 786440 | tf_op jit(solution)/shard_map/ppermute | solution.py:260
  11.0 32.3 %all-to-all-start = ((bf16[16,2,128,128]{3,2,1,0:T(8,128)(2,1)}), bf16[16,2,128,128]{3,2,1,0:T(8,128)(2,1)}, u32[]{:S(2)}, u32[]{:S(2)}) async-start(bf16[16,2,128,128]{3,2,1,0:T(8,128)(2,1)} %bitcast.7), calls=%async_computation | async-start | bytes 2097152 | tf_op jit(solution)/shard_map/all_to_all | solution.py:299
  19.7 19.7 %collective-permute-start.13 = (bf16[3,256,256]{2,1,0:T(8,128)(2,1)S(1)}, bf16[3,256,256]{2,1,0:T(8,128)(2,1)S(1)}, u32[]{:S(2)}, u32[]{:S(2)}) collective-permute-start(bf16[3,256,256]{2,1,0:T(8,128)(2,1)S(1)} %get-tuple-element.33), channel_id=1, source_target_pairs={{0,16},{2,18},{4,20},{6,22},{8,24},{10,26},{12,28},{14,30},{16,0},... | collective-permute-start | bytes 1179656 | tf_op jit(solution)/shard_map/ppermute | solution.py:265
  22.6 20.6 %copy-start = (bf16[2,128,512]{2,1,0:T(8,128)(2,1)S(1)}, bf16[2,128,512]{2,1,0:T(8,128)(2,1)}, u32[]{:S(2)}) copy-start(bf16[2,128,512]{2,1,0:T(8,128)(2,1)} %join.1.refs_0_) | copy-start | bytes 786436
  22.6 7.9 %collective-permute-start.1 = (bf16[2,128,512]{2,1,0:T(8,128)(2,1)}, bf16[2,128,512]{2,1,0:T(8,128)(2,1)S(1)}, u32[]{:S(2)}, u32[]{:S(2)}) collective-permute-start(bf16[2,128,512]{2,1,0:T(8,128)(2,1)} %join.1.refs_0_), channel_id=1, source_target_pairs={{0,64},{64,128},{128,192},{1,65},{65,129},{129,193},{2,66},{66,130... | collective-permute-start | bytes 786440 | tf_op jit(solution)/shard_map/ppermute | solution.py:285
  26.1 16.1 %collective-permute-start.17 = (bf16[256,256]{1,0:T(8,128)(2,1)S(1)}, bf16[256,256]{1,0:T(8,128)(2,1)S(1)}, u32[]{:S(2)}, u32[]{:S(2)}) collective-permute-start(bf16[256,256]{1,0:T(8,128)(2,1)S(1)} %get-tuple-element.26), channel_id=1, source_target_pairs={{0,130},{64,194},{128,0},{192,64},{2,128},{66,192},{130,2},{194,66... | collective-permute-start | bytes 393224 | tf_op jit(solution)/shard_map/ppermute | solution.py:261
  30.6 15.1 %collective-permute-start.3 = (bf16[2,128,512]{2,1,0:T(8,128)(2,1)S(1)}, bf16[2,128,512]{2,1,0:T(8,128)(2,1)S(1)}, u32[]{:S(2)}, u32[]{:S(2)}) collective-permute-start(bf16[2,128,512]{2,1,0:T(8,128)(2,1)S(1)} %collective-permute-done.1.refs_2_), channel_id=1, source_target_pairs={{0,64},{64,128},{128,192},{1,65},{65,129},{129,193},{2,66},{66,130... | collective-permute-start | bytes 786440 | tf_op jit(solution)/shard_map/ppermute | solution.py:285
  39.5 31.4 %collective-permute-start.16 = (bf16[2,3,256,256]{3,2,1,0:T(8,128)(2,1)S(1)}, bf16[2,3,256,256]{3,2,1,0:T(8,128)(2,1)S(1)}, u32[]{:S(2)}, u32[]{:S(2)}) collective-permute-start(bf16[2,3,256,256]{3,2,1,0:T(8,128)(2,1)S(1)} %pad_maximum_fusion.1.refs_0_), channel_id=1, source_target_pairs={{0,12},{2,14},{4,0},{6,2},{8,4},{10,6},{12,8},{14,10},{16,28},{18,... | collective-permute-start | bytes 2359304 | tf_op jit(solution)/shard_map/ppermute | solution.py:267
  43.2 31.2 %copy-start.2 = (bf16[1,128,2048]{2,1,0:T(8,128)(2,1)S(1)}, bf16[1,128,2048]{2,1,0:T(8,128)(2,1)}, u32[]{:S(2)}) copy-start(bf16[1,128,2048]{2,1,0:T(8,128)(2,1)} %param.6) | copy-start | bytes 1572868
  43.2 22.8 %collective-permute-start.18 = (bf16[3,256,256]{2,1,0:T(8,128)(2,1)}, bf16[3,256,256]{2,1,0:T(8,128)(2,1)}, u32[]{:S(2)}, u32[]{:S(2)}) collective-permute-start(bf16[3,256,256]{2,1,0:T(8,128)(2,1)} %get-tuple-element.31), channel_id=1, source_target_pairs={{0,4},{2,6},{4,0},{6,2},{8,12},{10,14},{12,8},{14,10},{16,20},{18,... | collective-permute-start | bytes 1179656 | tf_op jit(solution)/shard_map/ppermute | solution.py:265
  43.2 9.8 %collective-permute-start = (bf16[2,128,512]{2,1,0:T(8,128)(2,1)S(1)}, bf16[2,128,512]{2,1,0:T(8,128)(2,1)S(1)}, u32[]{:S(2)}, u32[]{:S(2)}) collective-permute-start(bf16[2,128,512]{2,1,0:T(8,128)(2,1)S(1)} %copy-done), channel_id=1, source_target_pairs={{0,1},{1,0},{2,3},{3,2},{4,5},{5,4},{6,7},{7,6},{8,9},{9,8},{10,11... | collective-permute-start | bytes 786440 | tf_op jit(solution)/shard_map/ppermute | solution.py:286
  45.7 20.3 %collective-permute-start.5 = (bf16[2,128,512]{2,1,0:T(8,128)(2,1)S(1)}, bf16[2,128,512]{2,1,0:T(8,128)(2,1)S(1)}, u32[]{:S(2)}, u32[]{:S(2)}) collective-permute-start(bf16[2,128,512]{2,1,0:T(8,128)(2,1)S(1)} %collective-permute-done.3.refs_4_), channel_id=1, source_target_pairs={{0,64},{64,128},{128,192},{1,65},{65,129},{129,193},{2,66},{66,130... | collective-permute-start | bytes 786440 | tf_op jit(solution)/shard_map/ppermute | solution.py:285
  49.9 24.0 %collective-permute-start.8 = (bf16[16,128,128]{2,1,0:T(8,128)(2,1)}, bf16[16,128,128]{2,1,0:T(8,128)(2,1)}, u32[]{:S(2)}, u32[]{:S(2)}) collective-permute-start(bf16[16,128,128]{2,1,0:T(8,128)(2,1)} %get-tuple-element.16), channel_id=1, source_target_pairs={{0,2},{2,0},{4,6},{6,4},{8,10},{10,8},{12,14},{14,12},{16,18},{18,... | collective-permute-start | bytes 1572872 | tf_op jit(solution)/shard_map/ppermute | solution.py:310
  53.0 14.8 %collective-permute-start.2 = (bf16[2,128,512]{2,1,0:T(8,128)(2,1)S(1)}, bf16[2,128,512]{2,1,0:T(8,128)(2,1)}, u32[]{:S(2)}, u32[]{:S(2)}) collective-permute-start(bf16[2,128,512]{2,1,0:T(8,128)(2,1)S(1)} %collective-permute-done.1.refs_2_), channel_id=1, source_target_pairs={{0,1},{1,0},{2,3},{3,2},{4,5},{5,4},{6,7},{7,6},{8,9},{9,8},{10,11... | collective-permute-start | bytes 786440 | tf_op jit(solution)/shard_map/ppermute | solution.py:286
  66.0 4.9 %collective-permute-start.4 = (bf16[2,128,512]{2,1,0:T(8,128)(2,1)S(1)}, bf16[2,128,512]{2,1,0:T(8,128)(2,1)}, u32[]{:S(2)}, u32[]{:S(2)}) collective-permute-start(bf16[2,128,512]{2,1,0:T(8,128)(2,1)S(1)} %collective-permute-done.3.refs_4_), channel_id=1, source_target_pairs={{0,1},{1,0},{2,3},{3,2},{4,5},{5,4},{6,7},{7,6},{8,9},{9,8},{10,11... | collective-permute-start | bytes 786440 | tf_op jit(solution)/shard_map/ppermute | solution.py:286
  66.0 5.0 %collective-permute-start.6 = (bf16[2,128,512]{2,1,0:T(8,128)(2,1)S(1)}, bf16[2,128,512]{2,1,0:T(8,128)(2,1)}, u32[]{:S(2)}, u32[]{:S(2)}) collective-permute-start(bf16[2,128,512]{2,1,0:T(8,128)(2,1)S(1)} %collective-permute-done.5.refs_6_), channel_id=1, source_target_pairs={{0,1},{1,0},{2,3},{3,2},{4,5},{5,4},{6,7},{7,6},{8,9},{9,8},{10,11... | collective-permute-start | bytes 786440 | tf_op jit(solution)/shard_map/ppermute | solution.py:286
  67.8 22.1 %collective-permute-start.15 = (bf16[2,3,256,256]{3,2,1,0:T(8,128)(2,1)S(1)}, bf16[2,3,256,256]{3,2,1,0:T(8,128)(2,1)S(1)}, u32[]{:S(2)}, u32[]{:S(2)}) collective-permute-start(bf16[2,3,256,256]{3,2,1,0:T(8,128)(2,1)S(1)} %pad_maximum_fusion.1.refs_0_), channel_id=1, source_target_pairs={{0,8},{2,10},{4,12},{6,14},{8,0},{10,2},{12,4},{14,6},{16,24},{18,... | collective-permute-start | bytes 2359304 | tf_op jit(solution)/shard_map/ppermute | solution.py:267
  70.8 34.8 %collective-permute-start.14 = (bf16[2,3,256,256]{3,2,1,0:T(8,128)(2,1)S(1)}, bf16[2,3,256,256]{3,2,1,0:T(8,128)(2,1)S(1)}, u32[]{:S(2)}, u32[]{:S(2)}) collective-permute-start(bf16[2,3,256,256]{3,2,1,0:T(8,128)(2,1)S(1)} %pad_maximum_fusion.1.refs_0_), channel_id=1, source_target_pairs={{0,4},{2,6},{4,8},{6,10},{8,12},{10,14},{12,0},{14,2},{16,20},{18,... | collective-permute-start | bytes 2359304 | tf_op jit(solution)/shard_map/ppermute | solution.py:267
  70.8 36.0 %collective-permute-start.21 = (bf16[2,3,256,256]{3,2,1,0:T(8,128)(2,1)S(1)}, bf16[2,3,256,256]{3,2,1,0:T(8,128)(2,1)S(1)}, u32[]{:S(2)}, u32[]{:S(2)}) collective-permute-start(bf16[2,3,256,256]{3,2,1,0:T(8,128)(2,1)S(1)} %pad_maximum_fusion.2.refs_4_), channel_id=1, source_target_pairs={{0,48},{2,50},{4,52},{6,54},{8,56},{10,58},{12,60},{14,62},{16,0},... | collective-permute-start | bytes 2359304 | tf_op jit(solution)/shard_map/ppermute | solution.py:267
  71.0 35.9 %collective-permute-start.20 = (bf16[2,3,256,256]{3,2,1,0:T(8,128)(2,1)S(1)}, bf16[2,3,256,256]{3,2,1,0:T(8,128)(2,1)S(1)}, u32[]{:S(2)}, u32[]{:S(2)}) collective-permute-start(bf16[2,3,256,256]{3,2,1,0:T(8,128)(2,1)S(1)} %pad_maximum_fusion.2.refs_4_), channel_id=1, source_target_pairs={{0,32},{2,34},{4,36},{6,38},{8,40},{10,42},{12,44},{14,46},{16,48}... | collective-permute-start | bytes 2359304 | tf_op jit(solution)/shard_map/ppermute | solution.py:267
  73.8 34.7 %collective-permute-start.19 = (bf16[2,3,256,256]{3,2,1,0:T(8,128)(2,1)S(1)}, bf16[2,3,256,256]{3,2,1,0:T(8,128)(2,1)S(1)}, u32[]{:S(2)}, u32[]{:S(2)}) collective-permute-start(bf16[2,3,256,256]{3,2,1,0:T(8,128)(2,1)S(1)} %pad_maximum_fusion.2.refs_4_), channel_id=1, source_target_pairs={{0,16},{2,18},{4,20},{6,22},{8,24},{10,26},{12,28},{14,30},{16,32}... | collective-permute-start | bytes 2359304 | tf_op jit(solution)/shard_map/ppermute | solution.py:267
  74.4 8.7 %copy-start.3 = (bf16[16,1,128,128]{3,2,1,0:T(8,128)(2,1)S(1)}, bf16[16,1,128,128]{3,2,1,0:T(8,128)(2,1)}, u32[]{:S(2)}) copy-start(bf16[16,1,128,128]{3,2,1,0:T(8,128)(2,1)} %get-tuple-element.28) | copy-start | bytes 1572868
  83.1 25.4 %copy-start.1 = (bf16[2048,512]{1,0:T(8,128)(2,1)S(1)}, bf16[2048,512]{1,0:T(8,128)(2,1)}, u32[]{:S(2)}) copy-start(bf16[2048,512]{1,0:T(8,128)(2,1)} %own.1) | copy-start | bytes 6291460
  89.8 18.7 %collective-permute-start.9 = (bf16[2,4,2,128,128]{4,3,2,1,0:T(8,128)(2,1)S(1)}, bf16[2,4,2,128,128]{4,3,2,1,0:T(8,128)(2,1)S(1)}, u32[]{:S(2)}, u32[]{:S(2)}) collective-permute-start(bf16[2,4,2,128,128]{4,3,2,1,0:T(8,128)(2,1)S(1)} %fusion.1), channel_id=1, source_target_pairs={{0,1},{1,0},{2,3},{3,2},{4,5},{5,4},{6,7},{7,6},{8,9},{9,8},{10,11... | collective-permute-start | bytes 1572872 | tf_op jit(solution)/shard_map/ppermute | solution.py:313
  105.7 2.9 %collective-permute-start.7 = (bf16[128,2048]{1,0:T(8,128)(2,1)S(1)}, bf16[128,2048]{1,0:T(8,128)(2,1)S(1)}, u32[]{:S(2)}, u32[]{:S(2)}) collective-permute-start(bf16[128,2048]{1,0:T(8,128)(2,1)S(1)} %get-tuple-element.15.mine), channel_id=1, source_target_pairs={{0,1},{1,0},{2,3},{3,2},{4,5},{5,4},{6,7},{7,6},{8,9},{9,8},{10,11... | collective-permute-start | bytes 1572872 | tf_op jit(solution)/shard_map/ppermute | solution.py:317
  115.0 2.0 %collective-permute-start.22 = (bf16[128,2048]{1,0:T(8,128)(2,1)S(1)}, bf16[128,2048]{1,0:T(8,128)(2,1)S(1)}, u32[]{:S(2)}, u32[]{:S(2)}) collective-permute-start(bf16[128,2048]{1,0:T(8,128)(2,1)S(1)} %get-tuple-element.18), channel_id=1, source_target_pairs={{0,1},{1,0},{2,3},{3,2},{4,5},{5,4},{6,7},{7,6},{8,9},{9,8},{10,11... | collective-permute-start | bytes 1572872 | tf_op jit(solution)/shard_map/ppermute | solution.py:322
  123.9 2.7 %collective-permute-start.23 = (bf16[4,2,128,512]{3,2,1,0:T(8,128)(2,1)S(1)}, bf16[4,2,128,512]{3,2,1,0:T(8,128)(2,1)S(1)}, u32[]{:S(2)}, u32[]{:S(2)}) collective-permute-start(bf16[4,2,128,512]{3,2,1,0:T(8,128)(2,1)S(1)} %get-tuple-element.22), channel_id=1, source_target_pairs={{0,1},{1,0},{2,3},{3,2},{4,5},{5,4},{6,7},{7,6},{8,9},{9,8},{10,11... | collective-permute-start | bytes 3145736 | tf_op jit(solution)/shard_map/ppermute | solution.py:325
  126.8 2.7 %collective-permute-start.26 = (bf16[2,128,512]{2,1,0:T(8,128)(2,1)S(1)}, bf16[2,128,512]{2,1,0:T(8,128)(2,1)S(1)}, u32[]{:S(2)}, u32[]{:S(2)}) collective-permute-start(bf16[2,128,512]{2,1,0:T(8,128)(2,1)S(1)} %get-tuple-element.24), channel_id=1, source_target_pairs={{192,128},{193,129},{194,130},{195,131},{196,132},{197,133},{198,1... | collective-permute-start | bytes 786440 | tf_op jit(solution)/shard_map/ppermute | solution.py:328
  127.5 10.5 %collective-permute-start.24 = (bf16[2,128,512]{2,1,0:T(8,128)(2,1)S(1)}, bf16[2,128,512]{2,1,0:T(8,128)(2,1)S(1)}, u32[]{:S(2)}, u32[]{:S(2)}) collective-permute-start(bf16[2,128,512]{2,1,0:T(8,128)(2,1)S(1)} %get-tuple-element.23), channel_id=1, source_target_pairs={{64,0},{128,64},{192,128},{65,1},{129,65},{193,129},{66,2},{130,66... | collective-permute-start | bytes 786440 | tf_op jit(solution)/shard_map/ppermute | solution.py:329
  128.8 9.2 %collective-permute-start.25 = (bf16[2,128,512]{2,1,0:T(8,128)(2,1)S(1)}, bf16[2,128,512]{2,1,0:T(8,128)(2,1)S(1)}, u32[]{:S(2)}, u32[]{:S(2)}) collective-permute-start(bf16[2,128,512]{2,1,0:T(8,128)(2,1)S(1)} %get-tuple-element.25), channel_id=1, source_target_pairs={{192,64},{193,65},{194,66},{195,67},{196,68},{197,69},{198,70},{19... | collective-permute-start | bytes 786440 | tf_op jit(solution)/shard_map/ppermute | solution.py:330
  129.6 25.6 %collective-permute-start.27 = (bf16[2,128,512]{2,1,0:T(8,128)(2,1)S(1)}, bf16[2,128,512]{2,1,0:T(8,128)(2,1)S(1)}, u32[]{:S(2)}, u32[]{:S(2)}) collective-permute-start(bf16[2,128,512]{2,1,0:T(8,128)(2,1)S(1)} %fusion.2), channel_id=1, source_target_pairs={{128,0},{129,1},{130,2},{131,3},{132,4},{133,5},{134,6},{135,7},{1... | collective-permute-start | bytes 786440 | tf_op jit(solution)/shard_map/ppermute | solution.py:332

commit v2 on v1

--- a/solution.py
+++ b/solution.py
@@ -141,7 +141,7 @@
     )(info, q, *pieces)
 
 
-def project_body(info, mine, theirs, target_mine, target_theirs, own, *refs):
+def project_body(info, mine, theirs, kept, got, target_theirs, own, *refs):
     arrays, (part_mine, part_theirs), (weights, both, acc, sems) = refs[:8], refs[8:10], refs[10:]
     grp, rep, xi, yi, zh = info[0], info[1], info[2], info[3], info[4]
     copies = [pltpu.make_async_copy(own, weights.at[3], sems.at[16])]
@@ -170,7 +170,11 @@
         target = jnp.concatenate(
             [
                 jnp.concatenate(
-                    [target_mine[(c + zh) % 2, block, rep, c // 2], target_theirs[(c + zh) % 2, block, c // 2]], axis=0
+                    [
+                        jnp.where(zh == c % 2, kept[block, rep, c // 2], got[block, rep, c // 2]),
+                        target_theirs[(c + zh) % 2, block, c // 2],
+                    ],
+                    axis=0,
                 )
                 for c in range(4)
             ],
@@ -186,7 +190,7 @@
     part_theirs[...] = acc[ROWS:].astype(jnp.bfloat16)
 
 
-def project(info, mine, theirs, target_mine, target_theirs, own, arrays):
+def project(info, mine, theirs, kept, got, target_theirs, own, arrays):
     vmem = pl.BlockSpec(memory_space=pltpu.VMEM)
     hbm = pl.BlockSpec(memory_space=pltpu.HBM)
     return pl.pallas_call(
@@ -194,7 +198,7 @@
         grid_spec=pltpu.PrefetchScalarGridSpec(
             num_scalar_prefetch=1,
             grid=(1,),
-            in_specs=[vmem] * 4 + [hbm] * 9,
+            in_specs=[vmem] * 5 + [hbm] * 9,
             out_specs=[vmem, vmem],
             scratch_shapes=[
                 pltpu.VMEM((4, FEAT, 512), jnp.bfloat16),
@@ -207,7 +211,7 @@
         compiler_params=PARAMS,
         cost_estimate=pl.CostEstimate(flops=10**10, bytes_accessed=12 * 10**6, transcendentals=0),
         name="project",
-    )(info, mine, theirs, target_mine, target_theirs, own, *arrays)
+    )(info, mine, theirs, kept, got, target_theirs, own, *arrays)
 
 
 def backward_body(probs, part, got, wide, q, *refs):
@@ -282,7 +286,7 @@
         if d == 3:
             piece, give = lax.optimization_barrier((piece, give))
         if d:
-            piece = lax.ppermute(piece, "grp", up(1))
+            piece = lax.ppermute(piece, "grp", up(1)[d - 1 :])
         pieces += [piece, lax.ppermute(piece, "rep", SWAP)]
     return pieces, give
 
@@ -308,29 +312,25 @@
     give = lax.dynamic_index_in_dim(rows, 1 - zh, 1, keepdims=False)
     pieces, give = gather_keys(key_rows, value_rows, give)
     got = lax.ppermute(give, "tp", [(t, t ^ 1) for t in range(32)])
-    target_mine = jnp.stack([keep, got]).reshape(2, N_GRP, 2, 2, ROWS, HD)
-    give = lax.dynamic_index_in_dim(target_mine, 1 - rep, 2, keepdims=False)
+    kept, got = [a.reshape(N_GRP, 2, 2, ROWS, HD) for a in (keep, got)]
+    give = jnp.stack([lax.dynamic_index_in_dim(a, 1 - rep, 1, keepdims=False) for a in (kept, got)])
     target_theirs = lax.ppermute(give, "rep", SWAP)
 
     pieces = [pltpu.with_memory_space_constraint(a, pltpu.VMEM) for a in pieces]
     wide, low, probs = forward(info, query, pieces)
     theirs = lax.ppermute(low, "rep", SWAP)
-    theirs, target_mine, target_theirs = [
-        pltpu.with_memory_space_constraint(a, pltpu.VMEM) for a in (theirs, target_mine, target_theirs)
+    theirs, kept, got, target_theirs = [
+        pltpu.with_memory_space_constraint(a, pltpu.VMEM) for a in (theirs, kept, got, target_theirs)
     ]
-    part, give = project(info, low, theirs, target_mine, target_theirs, projection, arrays)
+    part, give = project(info, low, theirs, kept, got, target_theirs, projection, arrays)
     got = lax.ppermute(give, "rep", SWAP)
     got = pltpu.with_memory_space_constraint(got, pltpu.VMEM)
     grad_q, terms_mine, terms_theirs = backward(probs, part, got, wide, query, pieces)
     got = lax.ppermute(terms_theirs, "rep", SWAP)
     terms = [terms_mine[d].astype(jnp.float32) + got[d].astype(jnp.float32) for d in range(N_GRP)]
-    low_terms = [t.astype(jnp.bfloat16) for t in terms]
-    relayed = lax.ppermute(low_terms[3], "grp", [(3, 2)])
-    near = lax.ppermute(low_terms[1], "grp", down(1))
-    far = lax.ppermute(low_terms[2], "grp", [(3, 1)])
-    joined = (terms[2] + relayed.astype(jnp.float32)).astype(jnp.bfloat16)
-    joined = lax.ppermute(joined, "grp", [(2, 0)])
-    total = terms[0] + near.astype(jnp.float32) + far.astype(jnp.float32) + joined.astype(jnp.float32)
+    total = terms[0]
+    for d in (3, 2, 1):
+        total = total + lax.ppermute(terms[d].astype(jnp.bfloat16), "grp", down(d)).astype(jnp.float32)
     total = total.astype(jnp.bfloat16)
     return grad_q[None], total[0:1], total[1:2]
 

time: 159 us -> 162 us (1.019)
  waiting for transfers between devices: 72.6 us -> 81.1 us
  starting transfers between devices: 46.2 us -> 42.2 us
  other arithmetic: 8.34 us -> 6.05 us
    ppermute x7 -> x6, starting transfers between devices: 15.9 us -> 10.1 us  [the longest x3 6.22 us: gather_keys(): piece = lax.ppermute(piece, 'grp', up(1)[d - 1:])]
    ppermute x2, waiting for transfers between devices: 17.5 us -> 21.7 us  [spread_weights(): other = lax.ppermute(slab, 'tp', pair)]
    ppermute x7 -> x6, waiting for transfers between devices: 26.5 us -> 28.8 us  [the longest x3 26.6 us: step(): lax.ppermute(terms[d].astype(jnp.bfloat16), 'grp', down(d))]
    ppermute x6, waiting for transfers between devices: 23.1 us -> 25 us  [spread_weights(): arrays += [slab] + [lax.ppermute(slab, 'tp', far(d)) for d in (1, 2, 3)]]
    ppermute x1, starting transfers between devices: 3.11 us -> 4.77 us  [step(): got = lax.ppermute(give, 'tp', [(t, t ^ 1) for t in range(32)])]
  transfers between devices with their start and end apart: 29 -> 28, of which waited for: 11 -> 12; matrix products, arithmetic and copies ran while one was open for 7% -> 5% of each run, Pallas kernels for 7% -> 7%
where the time goes in v2:
time: 162 us; the launch traced here: 159 us
  waiting for transfers between devices  81.1 us (50%)
  starting transfers between devices  42.2 us (26%)
  Pallas kernels  24.3 us (15%)
  other arithmetic  6.05 us (4%)
  local copies, waits for them, and re-layouts  4.06 us (3%)
    ppermute x3, waiting for transfers between devices, step(): lax.ppermute(terms[d].astype(jnp.bfloat16), 'grp', down(d))  26.6 us
    ppermute x6, waiting for transfers between devices, spread_weights(): arrays += [slab] + [lax.ppermute(slab, 'tp', far(d)) for d in (1, 2, 3)]  25 us
    ppermute x2, waiting for transfers between devices, spread_weights(): other = lax.ppermute(slab, 'tp', pair)  21.7 us
    ppermute x6, starting transfers between devices, spread_weights(): arrays += [slab] + [lax.ppermute(slab, 'tp', far(d)) for d in (1, 2, 3)]  9.36 us
    pallas_call x1, Pallas kernels, forward(): pl.pallas_call(forward_body, grid_spec=pltpu.PrefetchScalarGridSpec(num_s...  9 us
    all_to_all x1, starting transfers between devices, step(): lax.all_to_all(rows, 'tp', split_axis=0, concat_axis=0, tiled=True, axis_...  7.45 us
    pallas_call x1, Pallas kernels, backward(): pl.pallas_call(backward_body, grid=(KV_HEADS,), in_specs=[pl.BlockSpec((N...  7.2 us
    pallas_call x1, Pallas kernels, project(): pl.pallas_call(project_body, grid_spec=pltpu.PrefetchScalarGridSpec(num_s...  6.42 us
  transfers between devices with their start and end apart: 28, of which 12 were waited for; matrix products, arithmetic and copies ran while one was open for 5% of the time, Pallas kernels for 7%

profile of v2, /device:TPU:4, one launch (start us, length us, event | category | flops | bytes accessed | tf_op | source)
XLA Modules:
  0.0 158.6 jit_solution(1299617000832010266)
XLA Ops:
  0.7 1.0 constant_dynamic-slice_fusion.2
  1.7 3.3 %collective-permute-start.12 = (bf16[256,256]{1,0:T(8,128)(2,1)S(1)}, bf16[256,256]{1,0:T(8,128)(2,1)S(1)}, u32[]{:S(2)}, u32[]{:S(2)}) collective-permute-start(bf16[256,256]{1,0:T(8,128)(2,1)S(1)} %get-tuple-element.27), channel_id=1, source_target_pairs={{0,128},{64,192},{128,2},{192,66},{2,130},{66,194},{130,0},{194,64... | collective-permute-start | bytes 393224 | tf_op jit(solution)/shard_map/ppermute | solution.py:265
  5.1 2.7 %collective-permute-start.11 = (bf16[2,256,256]{2,1,0:T(8,128)(2,1)S(1)}, bf16[2,256,256]{2,1,0:T(8,128)(2,1)S(1)}, u32[]{:S(2)}, u32[]{:S(2)}) collective-permute-start(bf16[2,256,256]{2,1,0:T(8,128)(2,1)S(1)} %pad_maximum_fusion.5), channel_id=1, source_target_pairs={{0,194},{64,0},{128,64},{192,128},{2,192},{66,2},{130,66},{194,130... | collective-permute-start | bytes 786440 | tf_op jit(solution)/shard_map/ppermute | solution.py:264
  7.8 0.0 collective-permute-start.10
  7.8 0.7 bitcast_convert_fusion
  8.5 2.5 %multiply_convert_fusion = bf16[32,128,128]{2,1,0:T(8,128)(2,1)} fusion(bf16[32,128,128]{2,1,0:T(8,128)(2,1)} %param.9, f32[32,128]{1,0:T(8,128)S(1)} %bitcast_convert_fusion), kind=kLoop, calls=%fused_computation | loop fusion | flops 1572864 | bytes 2113536 | tf_op jit(solution)/shard_map/convert_element_type | solution.py:301
  11.0 7.5 %all-to-all-start = ((bf16[16,2,128,128]{3,2,1,0:T(8,128)(2,1)}), bf16[16,2,128,128]{3,2,1,0:T(8,128)(2,1)}, u32[]{:S(2)}, u32[]{:S(2)}) async-start(bf16[16,2,128,128]{3,2,1,0:T(8,128)(2,1)} %bitcast.7), calls=%async_computation | async-start | bytes 2097152 | tf_op jit(solution)/shard_map/all_to_all | solution.py:303
  18.5 1.1 collective-permute-done.10
  19.6 0.0 collective-permute-done.12
  19.6 0.1 fusion.7
  19.7 1.3 collective-permute-start.13
  20.9 1.7 %join.1.refs_0_ = bf16[2,128,512]{2,1,0:T(8,128)(2,1)} custom-call(bf16[1,128,512]{2,1,0:T(8,128)(2,1)} %keys.1, bf16[1,128,512]{2,1,0:T(8,128)(2,1)} %values.1), custom_call_target="tpu_custom_call" | custom-call | tf_op jit(solution)/shard_map/join/pallas_call | solution.py:281
  22.6 3.5 %collective-permute-start.1 = (bf16[2,128,512]{2,1,0:T(8,128)(2,1)}, bf16[2,128,512]{2,1,0:T(8,128)(2,1)S(1)}, u32[]{:S(2)}, u32[]{:S(2)}) collective-permute-start(bf16[2,128,512]{2,1,0:T(8,128)(2,1)} %join.1.refs_0_), channel_id=1, source_target_pairs={{0,64},{64,128},{128,192},{1,65},{65,129},{129,193},{2,66},{66,130... | collective-permute-start | bytes 786440 | tf_op jit(solution)/shard_map/ppermute | solution.py:289
  26.1 2.2 %collective-permute-start.17 = (bf16[256,256]{1,0:T(8,128)(2,1)S(1)}, bf16[256,256]{1,0:T(8,128)(2,1)S(1)}, u32[]{:S(2)}, u32[]{:S(2)}) collective-permute-start(bf16[256,256]{1,0:T(8,128)(2,1)S(1)} %get-tuple-element.26), channel_id=1, source_target_pairs={{0,130},{64,194},{128,0},{192,64},{2,128},{66,192},{130,2},{194,66... | collective-permute-start | bytes 393224 | tf_op jit(solution)/shard_map/ppermute | solution.py:265
  28.4 2.2 %collective-permute-done.1.refs_2_ = bf16[2,128,512]{2,1,0:T(8,128)(2,1)S(1)} collective-permute-done((bf16[2,128,512]{2,1,0:T(8,128)(2,1)}, bf16[2,128,512]{2,1,0:T(8,128)(2,1)S(1)}, u32[]{:S(2)}, u32[]{:S(2)}) %collective-permute-start.1) | collective-permute-done | bytes 262176 | tf_op jit(solution)/shard_map/ppermute | solution.py:289
  30.6 1.4 collective-permute-start.3
  31.9 7.4 %collective-permute-done.13 = bf16[3,256,256]{2,1,0:T(8,128)(2,1)S(1)} collective-permute-done((bf16[3,256,256]{2,1,0:T(8,128)(2,1)S(1)}, bf16[3,256,256]{2,1,0:T(8,128)(2,1)S(1)}, u32[]{:S(2)}, u32[]{:S(2)}) %collective-permute-start.13) | collective-permute-done | bytes 393248 | tf_op jit(solution)/shard_map/ppermute | solution.py:269
  39.4 0.1 pad_maximum_fusion.refs_0_
  39.5 2.8 %collective-permute-start.16 = (bf16[2,3,256,256]{3,2,1,0:T(8,128)(2,1)S(1)}, bf16[2,3,256,256]{3,2,1,0:T(8,128)(2,1)S(1)}, u32[]{:S(2)}, u32[]{:S(2)}) collective-permute-start(bf16[2,3,256,256]{3,2,1,0:T(8,128)(2,1)S(1)} %pad_maximum_fusion.refs_0_), channel_id=1, source_target_pairs={{0,12},{2,14},{4,0},{6,2},{8,4},{10,6},{12,8},{14,10},{16,28},{18,... | collective-permute-start | bytes 2359304 | tf_op jit(solution)/shard_map/ppermute | solution.py:271
  42.2 1.0 fusion.6
  43.2 0.0 collective-permute-start.18
  43.2 0.0 copy-start.2
  43.2 2.2 %constant_dynamic-slice_fusion.1 = (bf16[16,1,128,128]{3,2,1,0:T(8,128)(2,1)S(1)}, bf16[16,128,128]{2,1,0:T(8,128)(2,1)}) fusion(bf16[16,2,128,128]{3,2,1,0:T(8,128)(2,1)} %all-to-all-done, s32[]{:T(128)S(6)} %select_n.49, s32[]{:T(128)S(6)} %select_n.48), kind=kLoop, calls=%fused_computation.22 | loop fusion | bytes 2097160 | tf_op jit(solution)/shard_map/jit(dynamic_index_in_dim)/dynamic_slice | solution.py:311
  45.4 0.0 collective-permute-done.3.refs_4_
  45.4 1.4 collective-permute-start.5
  46.8 4.8 %collective-permute-start.8 = (bf16[16,128,128]{2,1,0:T(8,128)(2,1)}, bf16[16,128,128]{2,1,0:T(8,128)(2,1)S(1)}, u32[]{:S(2)}, u32[]{:S(2)}) collective-permute-start(bf16[16,128,128]{2,1,0:T(8,128)(2,1)} %get-tuple-element.16), channel_id=1, source_target_pairs={{0,2},{2,0},{4,6},{6,4},{8,10},{10,8},{12,14},{14,12},{16,18},{18,... | collective-permute-start | bytes 1572872 | tf_op jit(solution)/shard_map/ppermute | solution.py:314
  51.5 0.0 collective-permute-done.refs_1_
  51.6 0.2 collective-permute-start.2
  51.7 14.2 %collective-permute-done.18 = bf16[3,256,256]{2,1,0:T(8,128)(2,1)} collective-permute-done((bf16[3,256,256]{2,1,0:T(8,128)(2,1)}, bf16[3,256,256]{2,1,0:T(8,128)(2,1)}, u32[]{:S(2)}, u32[]{:S(2)}) %collective-permute-start.18) | collective-permute-done | bytes 393248 | tf_op jit(solution)/shard_map/ppermute | solution.py:269
  66.0 0.5 collective-permute-start.6
  66.5 0.1 stack.74.info
  66.6 1.2 pad_maximum_fusion.1.refs_4_
  67.9 0.0 collective-permute-done.2.refs_3_
  67.9 3.1 %collective-permute-start.15 = (bf16[2,3,256,256]{3,2,1,0:T(8,128)(2,1)S(1)}, bf16[2,3,256,256]{3,2,1,0:T(8,128)(2,1)S(1)}, u32[]{:S(2)}, u32[]{:S(2)}) collective-permute-start(bf16[2,3,256,256]{3,2,1,0:T(8,128)(2,1)S(1)} %pad_maximum_fusion.refs_0_), channel_id=1, source_target_pairs={{0,8},{2,10},{4,12},{6,14},{8,0},{10,2},{12,4},{14,6},{16,24},{18,... | collective-permute-start | bytes 2359304 | tf_op jit(solution)/shard_map/ppermute | solution.py:271
  70.9 0.0 collective-permute-done.4.refs_5_
  70.9 0.0 collective-permute-start.14
  70.9 0.0 collective-permute-done.16.refs_3_
  70.9 0.1 collective-permute-start.21
  71.0 0.0 collective-permute-done.6.refs_7_
  71.0 2.9 %collective-permute-start.20 = (bf16[2,3,256,256]{3,2,1,0:T(8,128)(2,1)S(1)}, bf16[2,3,256,256]{3,2,1,0:T(8,128)(2,1)S(1)}, u32[]{:S(2)}, u32[]{:S(2)}) collective-permute-start(bf16[2,3,256,256]{3,2,1,0:T(8,128)(2,1)S(1)} %pad_maximum_fusion.1.refs_4_), channel_id=1, source_target_pairs={{0,32},{2,34},{4,36},{6,38},{8,40},{10,42},{12,44},{14,46},{16,48}... | collective-permute-start | bytes 2359304 | tf_op jit(solution)/shard_map/ppermute | solution.py:271
  73.9 0.6 collective-permute-start.19
  74.5 9.0 %attn_fwd.1 = (f32[128,2048]{1,0:T(8,128)S(1)}, bf16[128,2048]{1,0:T(8,128)(2,1)S(1)}, bf16[4,512,1024]{2,1,0:T(8,128)(2,1)S(1)}) custom-call(s32[5]{0:T(128)S(1)} %stack.74.info, bf16[128,2048]{1,0:T(8,128)(2,1)S(1)} %bitcast.47, bf16[2,128,512]{2,1,0:T(8,128)(2,1)S(1)} %copy-done, bf16[2,128,512]{2,1,0:T(8,128)(2,1)} %collective-permute-done.refs_1_, ...), custom_call_target="tpu_custom_call" | custom-call | flops 10000000000 | bytes 8000000 | tf_op jit(solution)/shard_map/attn_fwd/pallas_call | solution.py:120
  83.5 0.1 pad_maximum_fusion.2
  83.6 6.3 %collective-permute-done.15.refs_2_ = bf16[2,3,256,256]{3,2,1,0:T(8,128)(2,1)S(1)} collective-permute-done((bf16[2,3,256,256]{3,2,1,0:T(8,128)(2,1)S(1)}, bf16[2,3,256,256]{3,2,1,0:T(8,128)(2,1)S(1)}, u32[]{:S(2)}, u32[]{:S(2)}) %collective-permute-start.15) | collective-permute-done | bytes 786464 | tf_op jit(solution)/shard_map/ppermute | solution.py:271
  89.9 0.0 collective-permute-start.9
  89.9 15.8 %collective-permute-done.14.refs_1_ = bf16[2,3,256,256]{3,2,1,0:T(8,128)(2,1)S(1)} collective-permute-done((bf16[2,3,256,256]{3,2,1,0:T(8,128)(2,1)S(1)}, bf16[2,3,256,256]{3,2,1,0:T(8,128)(2,1)S(1)}, u32[]{:S(2)}, u32[]{:S(2)}) %collective-permute-start.14) | collective-permute-done | bytes 786464 | tf_op jit(solution)/shard_map/ppermute | solution.py:271
  105.8 0.0 collective-permute-start.7
  105.8 2.9 %collective-permute-done.19.refs_5_ = bf16[2,3,256,256]{3,2,1,0:T(8,128)(2,1)S(1)} collective-permute-done((bf16[2,3,256,256]{3,2,1,0:T(8,128)(2,1)S(1)}, bf16[2,3,256,256]{3,2,1,0:T(8,128)(2,1)S(1)}, u32[]{:S(2)}, u32[]{:S(2)}) %collective-permute-start.19) | collective-permute-done | bytes 786464 | tf_op jit(solution)/shard_map/ppermute | solution.py:271
  108.6 0.0 collective-permute-done.9.target_theirs
  108.7 6.4 %project.1 = (f32[128,2048]{1,0:T(8,128)S(1)}, bf16[128,2048]{1,0:T(8,128)(2,1)S(1)}) custom-call(s32[5]{0:T(128)S(1)} %stack.74.info, bf16[128,2048]{1,0:T(8,128)(2,1)S(1)} %get-tuple-element.15.mine, bf16[128,2048]{1,0:T(8,128)(2,1)S(1)} %collective-permute-done.7.theirs, bf16[4,2,2,128,128]{4,3,2,1,0:T(8,128)(2,1)S(1)} %bitcast.44, ...), custom_call_target="tpu_custom_call" | custom-call | flops 10000000000 | bytes 12000000 | tf_op jit(solution)/shard_map/project/pallas_call | solution.py:196
  115.1 0.1 collective-permute-start.22
  115.2 1.9 %collective-permute-done.22.got = bf16[128,2048]{1,0:T(8,128)(2,1)S(1)} collective-permute-done((bf16[128,2048]{1,0:T(8,128)(2,1)S(1)}, bf16[128,2048]{1,0:T(8,128)(2,1)S(1)}, u32[]{:S(2)}, u32[]{:S(2)}) %collective-permute-start.22) | collective-permute-done | bytes 524320 | tf_op jit(solution)/shard_map/ppermute | solution.py:326
  117.1 7.2 %attn_bwd.1 = (bf16[128,2048]{1,0:T(8,128)(2,1)}, bf16[4,2,128,512]{3,2,1,0:T(8,128)(2,1)S(1)}, bf16[4,2,128,512]{3,2,1,0:T(8,128)(2,1)S(1)}) custom-call(bf16[4,512,1024]{2,1,0:T(8,128)(2,1)S(1)} %get-tuple-element.14.probs, f32[128,2048]{1,0:T(8,128)S(1)} %get-tuple-element.17.part, bf16[128,2048]{1,0:T(8,128)(2,1)S(1)} %collective-permute-done.22.got, ...), custom_call_target="tpu_custom_call" | custom-call | flops 10000000000 | bytes 8000000 | tf_op jit(solution)/shard_map/attn_bwd/pallas_call | solution.py:241
  124.3 0.1 collective-permute-start.23
  124.4 2.5 %collective-permute-done.23 = bf16[4,2,128,512]{3,2,1,0:T(8,128)(2,1)S(1)} collective-permute-done((bf16[4,2,128,512]{3,2,1,0:T(8,128)(2,1)S(1)}, bf16[4,2,128,512]{3,2,1,0:T(8,128)(2,1)S(1)}, u32[]{:S(2)}, u32[]{:S(2)}) %collective-permute-start.23) | collective-permute-done | bytes 1048608 | tf_op jit(solution)/shard_map/ppermute | solution.py:329
  126.9 0.2 fusion.3
  127.2 1.3 collective-permute-start.24
  128.5 1.3 collective-permute-start.26
  129.8 1.3 collective-permute-start.25
  131.1 11.0 %collective-permute-done.24 = bf16[2,128,512]{2,1,0:T(8,128)(2,1)S(1)} collective-permute-done((bf16[2,128,512]{2,1,0:T(8,128)(2,1)S(1)}, bf16[2,128,512]{2,1,0:T(8,128)(2,1)S(1)}, u32[]{:S(2)}, u32[]{:S(2)}) %collective-permute-start.24) | collective-permute-done | bytes 262176 | tf_op jit(solution)/shard_map/ppermute | solution.py:333
  142.0 2.3 %collective-permute-done.26 = bf16[2,128,512]{2,1,0:T(8,128)(2,1)S(1)} collective-permute-done((bf16[2,128,512]{2,1,0:T(8,128)(2,1)S(1)}, bf16[2,128,512]{2,1,0:T(8,128)(2,1)S(1)}, u32[]{:S(2)}, u32[]{:S(2)}) %collective-permute-start.26) | collective-permute-done | bytes 262176 | tf_op jit(solution)/shard_map/ppermute | solution.py:333
  144.3 13.4 %collective-permute-done.25 = bf16[2,128,512]{2,1,0:T(8,128)(2,1)S(1)} collective-permute-done((bf16[2,128,512]{2,1,0:T(8,128)(2,1)S(1)}, bf16[2,128,512]{2,1,0:T(8,128)(2,1)S(1)}, u32[]{:S(2)}, u32[]{:S(2)}) %collective-permute-start.25) | collective-permute-done | bytes 262176 | tf_op jit(solution)/shard_map/ppermute | solution.py:333
  157.7 0.2 fusion.2
  157.9 0.7 fusion.8
  (24 shorter events, 0.2 us)
Async XLA Ops:
  1.7 17.9 %collective-permute-start.12 = (bf16[256,256]{1,0:T(8,128)(2,1)S(1)}, bf16[256,256]{1,0:T(8,128)(2,1)S(1)}, u32[]{:S(2)}, u32[]{:S(2)}) collective-permute-start(bf16[256,256]{1,0:T(8,128)(2,1)S(1)} %get-tuple-element.27), channel_id=1, source_target_pairs={{0,128},{64,192},{128,2},{192,66},{2,130},{66,194},{130,0},{194,64... | collective-permute-start | bytes 393224 | tf_op jit(solution)/shard_map/ppermute | solution.py:265
  5.1 13.4 %collective-permute-start.11 = (bf16[2,256,256]{2,1,0:T(8,128)(2,1)S(1)}, bf16[2,256,256]{2,1,0:T(8,128)(2,1)S(1)}, u32[]{:S(2)}, u32[]{:S(2)}) collective-permute-start(bf16[2,256,256]{2,1,0:T(8,128)(2,1)S(1)} %pad_maximum_fusion.5), channel_id=1, source_target_pairs={{0,194},{64,0},{128,64},{192,128},{2,192},{66,2},{130,66},{194,130... | collective-permute-start | bytes 786440 | tf_op jit(solution)/shard_map/ppermute | solution.py:264
  7.8 11.8 %collective-permute-start.10 = (bf16[2,256,256]{2,1,0:T(8,128)(2,1)S(1)}, bf16[2,256,256]{2,1,0:T(8,128)(2,1)S(1)}, u32[]{:S(2)}, u32[]{:S(2)}) collective-permute-start(bf16[2,256,256]{2,1,0:T(8,128)(2,1)S(1)} %pad_maximum_fusion.5), channel_id=1, source_target_pairs={{0,64},{64,128},{128,192},{192,2},{2,66},{66,130},{130,194},{194,0... | collective-permute-start | bytes 786440 | tf_op jit(solution)/shard_map/ppermute | solution.py:264
  11.0 32.2 %all-to-all-start = ((bf16[16,2,128,128]{3,2,1,0:T(8,128)(2,1)}), bf16[16,2,128,128]{3,2,1,0:T(8,128)(2,1)}, u32[]{:S(2)}, u32[]{:S(2)}) async-start(bf16[16,2,128,128]{3,2,1,0:T(8,128)(2,1)} %bitcast.7), calls=%async_computation | async-start | bytes 2097152 | tf_op jit(solution)/shard_map/all_to_all | solution.py:303
  19.7 19.7 %collective-permute-start.13 = (bf16[3,256,256]{2,1,0:T(8,128)(2,1)S(1)}, bf16[3,256,256]{2,1,0:T(8,128)(2,1)S(1)}, u32[]{:S(2)}, u32[]{:S(2)}) collective-permute-start(bf16[3,256,256]{2,1,0:T(8,128)(2,1)S(1)} %get-tuple-element.33), channel_id=1, source_target_pairs={{0,16},{2,18},{4,20},{6,22},{8,24},{10,26},{12,28},{14,30},{16,0},... | collective-permute-start | bytes 1179656 | tf_op jit(solution)/shard_map/ppermute | solution.py:269
  22.6 20.6 %copy-start = (bf16[2,128,512]{2,1,0:T(8,128)(2,1)S(1)}, bf16[2,128,512]{2,1,0:T(8,128)(2,1)}, u32[]{:S(2)}) copy-start(bf16[2,128,512]{2,1,0:T(8,128)(2,1)} %join.1.refs_0_) | copy-start | bytes 786436
  22.6 7.9 %collective-permute-start.1 = (bf16[2,128,512]{2,1,0:T(8,128)(2,1)}, bf16[2,128,512]{2,1,0:T(8,128)(2,1)S(1)}, u32[]{:S(2)}, u32[]{:S(2)}) collective-permute-start(bf16[2,128,512]{2,1,0:T(8,128)(2,1)} %join.1.refs_0_), channel_id=1, source_target_pairs={{0,64},{64,128},{128,192},{1,65},{65,129},{129,193},{2,66},{66,130... | collective-permute-start | bytes 786440 | tf_op jit(solution)/shard_map/ppermute | solution.py:289
  26.1 16.1 %collective-permute-start.17 = (bf16[256,256]{1,0:T(8,128)(2,1)S(1)}, bf16[256,256]{1,0:T(8,128)(2,1)S(1)}, u32[]{:S(2)}, u32[]{:S(2)}) collective-permute-start(bf16[256,256]{1,0:T(8,128)(2,1)S(1)} %get-tuple-element.26), channel_id=1, source_target_pairs={{0,130},{64,194},{128,0},{192,64},{2,128},{66,192},{130,2},{194,66... | collective-permute-start | bytes 393224 | tf_op jit(solution)/shard_map/ppermute | solution.py:265
  30.6 14.8 %copy-start.3 = (bf16[2,128,512]{2,1,0:T(8,128)(2,1)}, bf16[2,128,512]{2,1,0:T(8,128)(2,1)S(1)}, u32[]{:S(2)}) copy-start(bf16[2,128,512]{2,1,0:T(8,128)(2,1)S(1)} %collective-permute-done.1.refs_2_) | copy-start | bytes 786436
  30.6 14.8 %collective-permute-start.3 = (bf16[2,128,512]{2,1,0:T(8,128)(2,1)S(1)}, bf16[2,128,512]{2,1,0:T(8,128)(2,1)}, u32[]{:S(2)}, u32[]{:S(2)}) collective-permute-start(bf16[2,128,512]{2,1,0:T(8,128)(2,1)S(1)} %collective-permute-done.1.refs_2_), channel_id=1, source_target_pairs={{64,128},{128,192},{65,129},{129,193},{66,130},{130,194},{67,131},... | collective-permute-start | bytes 786440 | tf_op jit(solution)/shard_map/ppermute | solution.py:289
  39.5 31.5 %collective-permute-start.16 = (bf16[2,3,256,256]{3,2,1,0:T(8,128)(2,1)S(1)}, bf16[2,3,256,256]{3,2,1,0:T(8,128)(2,1)S(1)}, u32[]{:S(2)}, u32[]{:S(2)}) collective-permute-start(bf16[2,3,256,256]{3,2,1,0:T(8,128)(2,1)S(1)} %pad_maximum_fusion.refs_0_), channel_id=1, source_target_pairs={{0,12},{2,14},{4,0},{6,2},{8,4},{10,6},{12,8},{14,10},{16,28},{18,... | collective-permute-start | bytes 2359304 | tf_op jit(solution)/shard_map/ppermute | solution.py:271
  43.2 22.8 %collective-permute-start.18 = (bf16[3,256,256]{2,1,0:T(8,128)(2,1)}, bf16[3,256,256]{2,1,0:T(8,128)(2,1)}, u32[]{:S(2)}, u32[]{:S(2)}) collective-permute-start(bf16[3,256,256]{2,1,0:T(8,128)(2,1)} %get-tuple-element.31), channel_id=1, source_target_pairs={{0,4},{2,6},{4,0},{6,2},{8,12},{10,14},{12,8},{14,10},{16,20},{18,... | collective-permute-start | bytes 1179656 | tf_op jit(solution)/shard_map/ppermute | solution.py:269
  43.2 8.4 %collective-permute-start = (bf16[2,128,512]{2,1,0:T(8,128)(2,1)S(1)}, bf16[2,128,512]{2,1,0:T(8,128)(2,1)}, u32[]{:S(2)}, u32[]{:S(2)}) collective-permute-start(bf16[2,128,512]{2,1,0:T(8,128)(2,1)S(1)} %copy-done), channel_id=1, source_target_pairs={{0,1},{1,0},{2,3},{3,2},{4,5},{5,4},{6,7},{7,6},{8,9},{9,8},{10,11... | collective-permute-start | bytes 786440 | tf_op jit(solution)/shard_map/ppermute | solution.py:290
  43.2 31.3 %copy-start.2 = (bf16[1,128,2048]{2,1,0:T(8,128)(2,1)S(1)}, bf16[1,128,2048]{2,1,0:T(8,128)(2,1)}, u32[]{:S(2)}) copy-start(bf16[1,128,2048]{2,1,0:T(8,128)(2,1)} %param.6) | copy-start | bytes 1572868
  45.4 20.6 %collective-permute-start.5 = (bf16[2,128,512]{2,1,0:T(8,128)(2,1)}, bf16[2,128,512]{2,1,0:T(8,128)(2,1)}, u32[]{:S(2)}, u32[]{:S(2)}) collective-permute-start(bf16[2,128,512]{2,1,0:T(8,128)(2,1)} %collective-permute-done.3.refs_4_), channel_id=1, source_target_pairs={{128,192},{129,193},{130,194},{131,195},{132,196},{133,197},{134,1... | collective-permute-start | bytes 786440 | tf_op jit(solution)/shard_map/ppermute | solution.py:289
  46.8 27.1 %collective-permute-start.8 = (bf16[16,128,128]{2,1,0:T(8,128)(2,1)}, bf16[16,128,128]{2,1,0:T(8,128)(2,1)S(1)}, u32[]{:S(2)}, u32[]{:S(2)}) collective-permute-start(bf16[16,128,128]{2,1,0:T(8,128)(2,1)} %get-tuple-element.16), channel_id=1, source_target_pairs={{0,2},{2,0},{4,6},{6,4},{8,10},{10,8},{12,14},{14,12},{16,18},{18,... | collective-permute-start | bytes 1572872 | tf_op jit(solution)/shard_map/ppermute | solution.py:314
  51.6 16.3 %collective-permute-start.2 = (bf16[2,128,512]{2,1,0:T(8,128)(2,1)}, bf16[2,128,512]{2,1,0:T(8,128)(2,1)}, u32[]{:S(2)}, u32[]{:S(2)}) collective-permute-start(bf16[2,128,512]{2,1,0:T(8,128)(2,1)} %copy-done.3), channel_id=1, source_target_pairs={{0,1},{1,0},{2,3},{3,2},{4,5},{5,4},{6,7},{7,6},{8,9},{9,8},{10,11... | collective-permute-start | bytes 786440 | tf_op jit(solution)/shard_map/ppermute | solution.py:290
  66.0 4.9 %collective-permute-start.4 = (bf16[2,128,512]{2,1,0:T(8,128)(2,1)}, bf16[2,128,512]{2,1,0:T(8,128)(2,1)}, u32[]{:S(2)}, u32[]{:S(2)}) collective-permute-start(bf16[2,128,512]{2,1,0:T(8,128)(2,1)} %collective-permute-done.3.refs_4_), channel_id=1, source_target_pairs={{0,1},{1,0},{2,3},{3,2},{4,5},{5,4},{6,7},{7,6},{8,9},{9,8},{10,11... | collective-permute-start | bytes 786440 | tf_op jit(solution)/shard_map/ppermute | solution.py:290
  66.0 5.0 %collective-permute-start.6 = (bf16[2,128,512]{2,1,0:T(8,128)(2,1)}, bf16[2,128,512]{2,1,0:T(8,128)(2,1)}, u32[]{:S(2)}, u32[]{:S(2)}) collective-permute-start(bf16[2,128,512]{2,1,0:T(8,128)(2,1)} %collective-permute-done.5.refs_6_), channel_id=1, source_target_pairs={{0,1},{1,0},{2,3},{3,2},{4,5},{5,4},{6,7},{7,6},{8,9},{9,8},{10,11... | collective-permute-start | bytes 786440 | tf_op jit(solution)/shard_map/ppermute | solution.py:290
  66.6 7.9 %copy-start.4 = (bf16[2,128,512]{2,1,0:T(8,128)(2,1)S(1)}, bf16[2,128,512]{2,1,0:T(8,128)(2,1)}, u32[]{:S(2)}) copy-start(bf16[2,128,512]{2,1,0:T(8,128)(2,1)} %copy-done.3) | copy-start | bytes 786436
  67.9 22.1 %collective-permute-start.15 = (bf16[2,3,256,256]{3,2,1,0:T(8,128)(2,1)S(1)}, bf16[2,3,256,256]{3,2,1,0:T(8,128)(2,1)S(1)}, u32[]{:S(2)}, u32[]{:S(2)}) collective-permute-start(bf16[2,3,256,256]{3,2,1,0:T(8,128)(2,1)S(1)} %pad_maximum_fusion.refs_0_), channel_id=1, source_target_pairs={{0,8},{2,10},{4,12},{6,14},{8,0},{10,2},{12,4},{14,6},{16,24},{18,... | collective-permute-start | bytes 2359304 | tf_op jit(solution)/shard_map/ppermute | solution.py:271
  70.9 34.8 %collective-permute-start.14 = (bf16[2,3,256,256]{3,2,1,0:T(8,128)(2,1)S(1)}, bf16[2,3,256,256]{3,2,1,0:T(8,128)(2,1)S(1)}, u32[]{:S(2)}, u32[]{:S(2)}) collective-permute-start(bf16[2,3,256,256]{3,2,1,0:T(8,128)(2,1)S(1)} %pad_maximum_fusion.refs_0_), channel_id=1, source_target_pairs={{0,4},{2,6},{4,8},{6,10},{8,12},{10,14},{12,0},{14,2},{16,20},{18,... | collective-permute-start | bytes 2359304 | tf_op jit(solution)/shard_map/ppermute | solution.py:271
  70.9 34.8 %collective-permute-start.21 = (bf16[2,3,256,256]{3,2,1,0:T(8,128)(2,1)S(1)}, bf16[2,3,256,256]{3,2,1,0:T(8,128)(2,1)S(1)}, u32[]{:S(2)}, u32[]{:S(2)}) collective-permute-start(bf16[2,3,256,256]{3,2,1,0:T(8,128)(2,1)S(1)} %pad_maximum_fusion.1.refs_4_), channel_id=1, source_target_pairs={{0,48},{2,50},{4,52},{6,54},{8,56},{10,58},{12,60},{14,62},{16,0},... | collective-permute-start | bytes 2359304 | tf_op jit(solution)/shard_map/ppermute | solution.py:271
  71.0 34.7 %collective-permute-start.20 = (bf16[2,3,256,256]{3,2,1,0:T(8,128)(2,1)S(1)}, bf16[2,3,256,256]{3,2,1,0:T(8,128)(2,1)S(1)}, u32[]{:S(2)}, u32[]{:S(2)}) collective-permute-start(bf16[2,3,256,256]{3,2,1,0:T(8,128)(2,1)S(1)} %pad_maximum_fusion.1.refs_4_), channel_id=1, source_target_pairs={{0,32},{2,34},{4,36},{6,38},{8,40},{10,42},{12,44},{14,46},{16,48}... | collective-permute-start | bytes 2359304 | tf_op jit(solution)/shard_map/ppermute | solution.py:271
  73.9 34.7 %collective-permute-start.19 = (bf16[2,3,256,256]{3,2,1,0:T(8,128)(2,1)S(1)}, bf16[2,3,256,256]{3,2,1,0:T(8,128)(2,1)S(1)}, u32[]{:S(2)}, u32[]{:S(2)}) collective-permute-start(bf16[2,3,256,256]{3,2,1,0:T(8,128)(2,1)S(1)} %pad_maximum_fusion.1.refs_4_), channel_id=1, source_target_pairs={{0,16},{2,18},{4,20},{6,22},{8,24},{10,26},{12,28},{14,30},{16,32}... | collective-permute-start | bytes 2359304 | tf_op jit(solution)/shard_map/ppermute | solution.py:271
  74.5 34.1 %copy-start.1 = (bf16[2048,512]{1,0:T(8,128)(2,1)S(1)}, bf16[2048,512]{1,0:T(8,128)(2,1)}, u32[]{:S(2)}) copy-start(bf16[2048,512]{1,0:T(8,128)(2,1)} %own.1) | copy-start | bytes 6291460
  89.9 18.7 %collective-permute-start.9 = (bf16[2,4,2,128,128]{4,3,2,1,0:T(8,128)(2,1)S(1)}, bf16[2,4,2,128,128]{4,3,2,1,0:T(8,128)(2,1)S(1)}, u32[]{:S(2)}, u32[]{:S(2)}) collective-permute-start(bf16[2,4,2,128,128]{4,3,2,1,0:T(8,128)(2,1)S(1)} %pad_maximum_fusion.2), channel_id=1, source_target_pairs={{0,1},{1,0},{2,3},{3,2},{4,5},{5,4},{6,7},{7,6},{8,9},{9,8},{10,11... | collective-permute-start | bytes 1572872 | tf_op jit(solution)/shard_map/ppermute | solution.py:317
  105.8 2.9 %collective-permute-start.7 = (bf16[128,2048]{1,0:T(8,128)(2,1)S(1)}, bf16[128,2048]{1,0:T(8,128)(2,1)S(1)}, u32[]{:S(2)}, u32[]{:S(2)}) collective-permute-start(bf16[128,2048]{1,0:T(8,128)(2,1)S(1)} %get-tuple-element.15.mine), channel_id=1, source_target_pairs={{0,1},{1,0},{2,3},{3,2},{4,5},{5,4},{6,7},{7,6},{8,9},{9,8},{10,11... | collective-permute-start | bytes 1572872 | tf_op jit(solution)/shard_map/ppermute | solution.py:321
  115.1 2.0 %collective-permute-start.22 = (bf16[128,2048]{1,0:T(8,128)(2,1)S(1)}, bf16[128,2048]{1,0:T(8,128)(2,1)S(1)}, u32[]{:S(2)}, u32[]{:S(2)}) collective-permute-start(bf16[128,2048]{1,0:T(8,128)(2,1)S(1)} %get-tuple-element.18), channel_id=1, source_target_pairs={{0,1},{1,0},{2,3},{3,2},{4,5},{5,4},{6,7},{7,6},{8,9},{9,8},{10,11... | collective-permute-start | bytes 1572872 | tf_op jit(solution)/shard_map/ppermute | solution.py:326
  124.3 2.7 %collective-permute-start.23 = (bf16[4,2,128,512]{3,2,1,0:T(8,128)(2,1)S(1)}, bf16[4,2,128,512]{3,2,1,0:T(8,128)(2,1)S(1)}, u32[]{:S(2)}, u32[]{:S(2)}) collective-permute-start(bf16[4,2,128,512]{3,2,1,0:T(8,128)(2,1)S(1)} %get-tuple-element.22), channel_id=1, source_target_pairs={{0,1},{1,0},{2,3},{3,2},{4,5},{5,4},{6,7},{7,6},{8,9},{9,8},{10,11... | collective-permute-start | bytes 3145736 | tf_op jit(solution)/shard_map/ppermute | solution.py:329
  127.2 14.9 %collective-permute-start.24 = (bf16[2,128,512]{2,1,0:T(8,128)(2,1)S(1)}, bf16[2,128,512]{2,1,0:T(8,128)(2,1)S(1)}, u32[]{:S(2)}, u32[]{:S(2)}) collective-permute-start(bf16[2,128,512]{2,1,0:T(8,128)(2,1)S(1)} %get-tuple-element.23), channel_id=1, source_target_pairs={{192,0},{193,1},{194,2},{195,3},{196,4},{197,5},{198,6},{199,7},{2... | collective-permute-start | bytes 786440 | tf_op jit(solution)/shard_map/ppermute | solution.py:333
  128.5 15.9 %collective-permute-start.26 = (bf16[2,128,512]{2,1,0:T(8,128)(2,1)S(1)}, bf16[2,128,512]{2,1,0:T(8,128)(2,1)S(1)}, u32[]{:S(2)}, u32[]{:S(2)}) collective-permute-start(bf16[2,128,512]{2,1,0:T(8,128)(2,1)S(1)} %get-tuple-element.24), channel_id=1, source_target_pairs={{64,0},{128,64},{192,128},{65,1},{129,65},{193,129},{66,2},{130,66... | collective-permute-start | bytes 786440 | tf_op jit(solution)/shard_map/ppermute | solution.py:333
  129.8 27.9 %collective-permute-start.25 = (bf16[2,128,512]{2,1,0:T(8,128)(2,1)S(1)}, bf16[2,128,512]{2,1,0:T(8,128)(2,1)S(1)}, u32[]{:S(2)}, u32[]{:S(2)}) collective-permute-start(bf16[2,128,512]{2,1,0:T(8,128)(2,1)S(1)} %get-tuple-element.25), channel_id=1, source_target_pairs={{128,0},{192,64},{129,1},{193,65},{130,2},{194,66},{131,3},{195,67... | collective-permute-start | bytes 786440 | tf_op jit(solution)/shard_map/ppermute | solution.py:333
